TPU v7x, 512 devices: a whole 4x8x8 slice. The times are simulated.
512 devices in a mesh: section: 16 (over z_hi, y), dp: 4 (over x), tensor: 8 (over z_lo, core).
Axes of the slice: x: 4, y: 8, z: 8 (z_hi: 2, z_lo: 4; z = z_hi * 4 + z_lo), core: 2. Of those that a mesh axis runs over, the one named last changes fastest.
Arguments:
- sent_out: bfloat16 [16, 2, 768, 4096], P('section', None, 'dp', 'tensor'), may hold values from -6 to 6
- sent_back: bfloat16 [16, 2, 768, 4096], P('section', None, 'dp', 'tensor'), may hold values from -6 to 6
- sent_grad: bfloat16 [16, 2, 768, 4096], P('section', None, 'dp', 'tensor'), may hold values from -6 to 6
- lengths: int32 [16, 4], P('section', 'dp'), may hold values from 48 to 192
- weight: bfloat16 [16, 4096, 4096], P('section', 'dp', 'tensor'), may hold values from -0.09375 to 0.09375
Outputs:
- emitted: bfloat16 [16, 2, 768, 4096], P('section', None, 'dp', 'tensor')
- rebuilt: bfloat16 [16, 2, 768, 4096], P('section', None, 'dp', 'tensor')
- input_grad: bfloat16 [16, 2, 768, 4096], P('section', None, 'dp', 'tensor')
- weight_grad: bfloat16 [16, 4096, 4096], P('section', 'dp', 'tensor')
All inputs are finite; a program needn't handle non-finite values.
Results may differ from a plain program's by a relative error of at most 0.0075.
Values may be sent and summed in bfloat16 or wider, within the bound.
No kernel may reach another device: no remote copies, remote signals or barrier semaphores. Data moves between devices by JAX's collectives and lax.ppermute only.
A program may use at most 64 MiB of HBM per device.

v0:
```python
import jax
import jax.numpy as jnp
from jax import lax
from jax.sharding import PartitionSpec as P


def shifted(block, axis, distance):
    devices = range(lax.axis_size(axis))
    route = [((i - distance) % len(devices), i) for i in devices]
    return lax.ppermute(block, axis, route)


def sent_to_all(x, axis):
    copies = jnp.broadcast_to(x, (lax.axis_size(axis), *x.shape))
    return lax.all_to_all(copies, axis, split_axis=0, concat_axis=0, tiled=True)


def laid_out(pieces, dim):
    pieces = jnp.moveaxis(pieces, 0, dim)
    dims = pieces.shape
    return pieces.reshape(*dims[:dim], dims[dim] * dims[dim + 1], *dims[dim + 2 :])


def collect(x, axis, dim):
    pieces = sent_to_all(x, axis)
    return laid_out(pieces, dim)


def across_rows(left, right):
    return lax.dot_general(
        left, right, (((0,), (0,)), ((), ())), preferred_element_type=jnp.float32
    )


def slope(hidden):
    sigma = jax.nn.sigmoid(hidden)
    return sigma * (1.0 + hidden * (1.0 - sigma))


def local(sent_out, sent_back, sent_grad, lengths, weight):
    token_rows = sent_out.shape[2]
    local_weight = weight[0]
    whole_weight = lax.all_gather(local_weight, "dp", axis=0, tiled=True)
    inbound = shifted(sent_out, "section", 1)
    upper_in = inbound[0, 0]
    lower_in = inbound[0, 1]
    upper_full = lax.all_gather(upper_in, "tensor", axis=1, tiled=True)
    pre = jnp.dot(upper_full, whole_weight, preferred_element_type=jnp.float32)
    upper_out = (lower_in.astype(jnp.float32) + jax.nn.silu(pre)).astype(jnp.bfloat16)
    emitted = jnp.stack([upper_out, upper_in])[None]
    back, incoming = shifted((sent_back, sent_grad), "section", -1)
    back_upper = back[0, 0]
    back_lower = back[0, 1]
    lower_full = collect(back_lower, "tensor", 1)
    pre_held = jnp.dot(lower_full, whole_weight, preferred_element_type=jnp.float32)
    rebuilt_lower = (back_upper.astype(jnp.float32) - jax.nn.silu(pre_held)).astype(jnp.bfloat16)
    rebuilt = jnp.stack([back_lower, rebuilt_lower])[None]
    keep = (jnp.arange(token_rows, dtype=jnp.int32) < lengths[0, 0])[:, None]
    zero = jnp.zeros((), jnp.bfloat16)
    dupper = jnp.where(keep, incoming[0, 0], zero)
    dlower = jnp.where(keep, incoming[0, 1], zero)
    hidden = (dupper.astype(jnp.float32) * slope(pre_held)).astype(jnp.bfloat16)
    terms = lax.dot_general(
        hidden, whole_weight, (((1,), (1,)), ((), ())), preferred_element_type=jnp.float32
    )
    through = lax.psum_scatter(
        terms.astype(jnp.bfloat16), "tensor", scatter_dimension=1, tiled=True
    ).astype(jnp.float32)
    dupper_in = (dlower.astype(jnp.float32) + through).astype(jnp.bfloat16)
    grads_out = jnp.stack([dupper_in, dupper])[None]
    held_share = lax.all_to_all(lower_full, "dp", split_axis=1, concat_axis=0, tiled=True)
    hidden_all = collect(hidden, "dp", 0)
    weight_grad = across_rows(held_share, hidden_all).astype(jnp.bfloat16)[None]
    rebuilt, grads_out, weight_grad = (rebuilt, grads_out, weight_grad)
    return (emitted, rebuilt, grads_out, weight_grad)


def solution(mesh):
    return jax.shard_map(
        local,
        mesh=mesh,
        in_specs=(
            P("section", None, "dp", "tensor"),
            P("section", None, "dp", "tensor"),
            P("section", None, "dp", "tensor"),
            P("section", "dp"),
            P("section", "dp", "tensor"),
        ),
        out_specs=(
            P("section", None, "dp", "tensor"),
            P("section", None, "dp", "tensor"),
            P("section", None, "dp", "tensor"),
            P("section", "dp", "tensor"),
        ),
        check_vma=False,
    )
```

profile of v0, /device:TPU:6, one launch (start us, length us, event | category | flops | bytes accessed | tf_op | source)
XLA Modules:
  0.0 175.0 jit_solution(11782850779910412422)
XLA Ops:
  7.2 0.0 all-gather.7.cloned.1.call-start
  7.2 0.7 all-gather.7.cloned.1.call-update
  7.9 13.8 %collective-permute-start.1 = (bf16[1,2,192,512]{3,2,1,0:T(8,128)(2,1)}, bf16[1,2,192,512]{3,2,1,0:T(8,128)(2,1)}, u32[]{:S(2)}, u32[]{:S(2)}) collective-permute-start(bf16[1,2,192,512]{3,2,1,0:T(8,128)(2,1)} %param.6), channel_id=1, source_target_pairs={{32,0},{64,32},{96,64},{128,96},{160,128},{192,160},{224,192},{256... | collective-permute-start | bytes 1179656 | tf_op jit(solution)/shard_map/ppermute | solution.py:10
  21.7 14.6 %collective-permute-done.1 = bf16[1,2,192,512]{3,2,1,0:T(8,128)(2,1)} collective-permute-done((bf16[1,2,192,512]{3,2,1,0:T(8,128)(2,1)}, bf16[1,2,192,512]{3,2,1,0:T(8,128)(2,1)}, u32[]{:S(2)}, u32[]{:S(2)}) %collective-permute-start.1) | collective-permute-done | bytes 393248 | tf_op jit(solution)/shard_map/ppermute | solution.py:10
  36.3 1.6 slice_bitcast_fusion.4
  37.9 1.3 broadcast_in_dim.40
  39.2 0.0 copy-start.6
  39.2 6.3 %all-to-all-start = ((bf16[8,192,512]{2,1,0:T(8,128)(2,1)}), bf16[8,192,512]{2,1,0:T(8,128)(2,1)S(1)}, u32[]{:S(2)}, u32[]{:S(2)}) async-start(bf16[8,192,512]{2,1,0:T(8,128)(2,1)} %broadcast_in_dim.40), calls=%async_computation | async-start | bytes 3145728 | tf_op jit(solution)/shard_map/all_to_all | solution.py:15
  45.6 0.0 all-gather.5.cloned.1.call-start
  45.6 0.0 copy-done.6
  45.6 1.9 %collective-permute-start = (bf16[1,2,192,512]{3,2,1,0:T(8,128)(2,1)S(1)}, bf16[1,2,192,512]{3,2,1,0:T(8,128)(2,1)S(1)}, u32[]{:S(2)}, u32[]{:S(2)}) collective-permute-start(bf16[1,2,192,512]{3,2,1,0:T(8,128)(2,1)S(1)} %copy-done.6), channel_id=1, source_target_pairs={{480,0},{0,32},{32,64},{64,96},{96,128},{128,160},{160,192},{192,2... | collective-permute-start | bytes 1179656 | tf_op jit(solution)/shard_map/ppermute | solution.py:10
  47.5 30.4 %collective-permute-done = bf16[1,2,192,512]{3,2,1,0:T(8,128)(2,1)S(1)} collective-permute-done((bf16[1,2,192,512]{3,2,1,0:T(8,128)(2,1)S(1)}, bf16[1,2,192,512]{3,2,1,0:T(8,128)(2,1)S(1)}, u32[]{:S(2)}, u32[]{:S(2)}) %collective-permute-start) | collective-permute-done | bytes 393248 | tf_op jit(solution)/shard_map/ppermute | solution.py:10
  77.9 0.7 copy-done.4
  78.7 0.8 fusion.16
  79.5 0.0 all-gather.5.cloned.1.call-update
  79.5 0.0 reduce-scatter.2.cloned.1.call-start
  79.5 1.9 %collective-permute-start.2 = (bf16[1,2,192,512]{3,2,1,0:T(8,128)(2,1)}, bf16[1,2,192,512]{3,2,1,0:T(8,128)(2,1)}, u32[]{:S(2)}, u32[]{:S(2)}) collective-permute-start(bf16[1,2,192,512]{3,2,1,0:T(8,128)(2,1)} %param.7), channel_id=1, source_target_pairs={{32,0},{64,32},{96,64},{128,96},{160,128},{192,160},{224,192},{256... | collective-permute-start | bytes 1179656 | tf_op jit(solution)/shard_map/ppermute | solution.py:10
  82.1 26.3 %all-to-all-done = bf16[8,192,512]{2,1,0:T(8,128)(2,1)S(1)} async-done(((bf16[8,192,512]{2,1,0:T(8,128)(2,1)}), bf16[8,192,512]{2,1,0:T(8,128)(2,1)S(1)}, u32[]{:S(2)}, u32[]{:S(2)}) %all-to-all-start) | async-done | bytes 1572896 | tf_op jit(solution)/shard_map/all_to_all | solution.py:15
  108.4 0.2 copy.16
  108.6 0.0 collective-permute-done.2
  108.6 0.0 all-gather.7.cloned.1.call-done
  108.6 0.0 copy-start
  108.6 3.6 %multiply_convert_fusion = (bf16[192,512]{1,0:T(8,128)(2,1)S(1)}, bf16[1,192,512]{2,1,0:T(8,128)(2,1)S(1)}) fusion(pred[192]{0:T(512)(128)(4,1)S(1)} %iota_compare_fusion, bf16[1,2,192,512]{3,2,1,0:T(8,128)(2,1)} %collective-permute-done.2, bf16[1,2,192,512]{3,2,1,0:T(8,128)(2,1)} %collective-permute-done.1, bf16[192,4096]{1,0:T(8,128)(2,1)S(1)} %bitcast.83, ...), kind=kOutput, calls=%fused_computation.18 | convolution fusion | flops 806780928 | bytes 6553792 | tf_op jit(solution)/shard_map/dot_general | solution.py:55
  112.2 0.0 copy-done
  112.3 2.7 %convolution_convert_fusion = bf16[192,4096]{1,0:T(8,128)(2,1)} fusion(bf16[192,512]{1,0:T(8,128)(2,1)S(1)} %get-tuple-element.16, bf16[1,4096,512]{2,1,0:T(8,128)(2,1)S(1)} %copy-done), kind=kOutput, calls=%fused_computation | convolution fusion | flops 806092800 | bytes 5963776 | tf_op jit(solution)/shard_map/dot_general | solution.py:63
  114.9 0.0 reduce-scatter.2.cloned.1.call-update
  115.0 0.9 copy.12
  115.8 1.1 all_to_all.20
  116.9 1.7 copy.14
  118.6 4.8 %all-to-all-start.2 = ((bf16[192,4,1024]{2,0,1:T(8,128)(2,1)}), bf16[192,4,1024]{2,0,1:T(8,128)(2,1)S(1)}, u32[]{:S(2)}, u32[]{:S(2)}) async-start(bf16[192,4,1024]{2,0,1:T(8,128)(2,1)} %copy.14), calls=%async_computation.3 | async-start | bytes 3145728 | tf_op jit(solution)/shard_map/all_to_all | solution.py:71
  123.3 1.7 bitcast_select_fusion
  125.1 15.5 %all-to-all-done.2 = bf16[192,4,1024]{2,0,1:T(8,128)(2,1)S(1)} async-done(((bf16[192,4,1024]{2,0,1:T(8,128)(2,1)}), bf16[192,4,1024]{2,0,1:T(8,128)(2,1)S(1)}, u32[]{:S(2)}, u32[]{:S(2)}) %all-to-all-start.2) | async-done | bytes 1572896 | tf_op jit(solution)/shard_map/all_to_all | solution.py:71
  140.6 0.9 broadcast_in_dim.47
  141.5 5.5 %all-to-all-start.1 = ((bf16[4,192,512]{2,1,0:T(8,128)(2,1)}), bf16[4,192,512]{2,1,0:T(8,128)(2,1)S(1)}, u32[]{:S(2)}, u32[]{:S(2)}) async-start(bf16[4,192,512]{2,1,0:T(8,128)(2,1)} %broadcast_in_dim.47), calls=%async_computation.2 | async-start | bytes 1572864 | tf_op jit(solution)/shard_map/all_to_all | solution.py:15
  147.1 0.0 copy-done.2
  147.1 0.8 maximum_bitcast_fusion.1
  147.9 0.0 copy-done.5
  147.9 3.7 %fusion.14 = bf16[1,192,512]{2,1,0:T(8,128)(2,1)S(1)} fusion(bf16[1,2,192,512]{3,2,1,0:T(8,128)(2,1)S(1)} %copy-done.5, bf16[1,4096,512]{2,1,0:T(8,128)(2,1)} %all-gather.7.cloned.1.call-done, bf16[1,1,192,4096]{3,2,1,0:T(8,128)(2,1)} %all-gather.5.cloned.1.call-done), kind=kOutput, calls=%fused_computation.27 | convolution fusion | flops 805994496 | bytes 6160384 | tf_op jit(solution)/shard_map/dot_general | solution.py:48
  151.6 0.0 copy-done.3
  151.6 0.8 maximum_bitcast_fusion
  152.4 2.6 %all-to-all-done.1 = bf16[4,192,512]{2,1,0:T(8,128)(2,1)S(1)} async-done(((bf16[4,192,512]{2,1,0:T(8,128)(2,1)}), bf16[4,192,512]{2,1,0:T(8,128)(2,1)S(1)}, u32[]{:S(2)}, u32[]{:S(2)}) %all-to-all-start.1) | async-done | bytes 786464 | tf_op jit(solution)/shard_map/all_to_all | solution.py:15
  155.1 1.0 fusion.7
  156.1 0.0 copy-start.1
  156.1 1.3 copy.15
  157.4 9.1 %reduce-scatter.2.cloned.1.call-done = bf16[192,512]{1,0:T(8,128)(2,1)} async-done(((bf16[192,4096]{1,0:T(8,128)(2,1)}), bf16[192,512]{1,0:T(8,128)(2,1)}) %reduce-scatter.2.cloned.1.call-update) | async-done | bytes 196624 | tf_op jit(solution)/shard_map/reduce_scatter | solution.py:66
  166.5 1.2 fusion.12
  167.6 0.0 copy-done.1
  167.7 0.8 maximum_bitcast_fusion.2
  (6 shorter events, 0.0 us)
Async XLA Ops:
  7.2 101.4 %all-gather.7.cloned.1.call-start = ((), (), s32[]{:S(2)}) async-start(), calls=%async_computation.6 | async-start | bytes 5242880 | tf_op jit(solution)/shard_map/all_gather | solution.py:43
  7.9 28.4 %collective-permute-start.1 = (bf16[1,2,192,512]{3,2,1,0:T(8,128)(2,1)}, bf16[1,2,192,512]{3,2,1,0:T(8,128)(2,1)}, u32[]{:S(2)}, u32[]{:S(2)}) collective-permute-start(bf16[1,2,192,512]{3,2,1,0:T(8,128)(2,1)} %param.6), channel_id=1, source_target_pairs={{32,0},{64,32},{96,64},{128,96},{160,128},{192,160},{224,192},{256... | collective-permute-start | bytes 1179656 | tf_op jit(solution)/shard_map/ppermute | solution.py:10
  39.2 6.4 %copy-start.6 = (bf16[1,2,192,512]{3,2,1,0:T(8,128)(2,1)S(1)}, bf16[1,2,192,512]{3,2,1,0:T(8,128)(2,1)}, u32[]{:S(2)}) copy-start(bf16[1,2,192,512]{3,2,1,0:T(8,128)(2,1)} %param.5) | copy-start | bytes 1179652
  39.2 69.2 %all-to-all-start = ((bf16[8,192,512]{2,1,0:T(8,128)(2,1)}), bf16[8,192,512]{2,1,0:T(8,128)(2,1)S(1)}, u32[]{:S(2)}, u32[]{:S(2)}) async-start(bf16[8,192,512]{2,1,0:T(8,128)(2,1)} %broadcast_in_dim.40), calls=%async_computation | async-start | bytes 3145728 | tf_op jit(solution)/shard_map/all_to_all | solution.py:15
  45.6 102.3 %all-gather.5.cloned.1.call-start = ((), (), s32[]{:S(2)}) async-start(), calls=%async_computation.5 | async-start | bytes 1769472 | tf_op jit(solution)/shard_map/all_gather | solution.py:47
  45.6 32.3 %collective-permute-start = (bf16[1,2,192,512]{3,2,1,0:T(8,128)(2,1)S(1)}, bf16[1,2,192,512]{3,2,1,0:T(8,128)(2,1)S(1)}, u32[]{:S(2)}, u32[]{:S(2)}) collective-permute-start(bf16[1,2,192,512]{3,2,1,0:T(8,128)(2,1)S(1)} %copy-done.6), channel_id=1, source_target_pairs={{480,0},{0,32},{32,64},{64,96},{96,128},{128,160},{160,192},{192,2... | collective-permute-start | bytes 1179656 | tf_op jit(solution)/shard_map/ppermute | solution.py:10
  77.9 0.7 copy-start.4
  79.5 87.0 %reduce-scatter.2.cloned.1.call-start = ((), (), s32[]{:S(2)}) async-start(), calls=%async_computation.4 | async-start | bytes 1769472 | tf_op jit(solution)/shard_map/reduce_scatter | solution.py:66
  79.5 29.0 %collective-permute-start.2 = (bf16[1,2,192,512]{3,2,1,0:T(8,128)(2,1)}, bf16[1,2,192,512]{3,2,1,0:T(8,128)(2,1)}, u32[]{:S(2)}, u32[]{:S(2)}) collective-permute-start(bf16[1,2,192,512]{3,2,1,0:T(8,128)(2,1)} %param.7), channel_id=1, source_target_pairs={{32,0},{64,32},{96,64},{128,96},{160,128},{192,160},{224,192},{256... | collective-permute-start | bytes 1179656 | tf_op jit(solution)/shard_map/ppermute | solution.py:10
  108.6 3.7 %copy-start = (bf16[1,4096,512]{2,1,0:T(8,128)(2,1)S(1)}, bf16[1,4096,512]{2,1,0:T(8,128)(2,1)}, u32[]{:S(2)}) copy-start(bf16[1,4096,512]{2,1,0:T(8,128)(2,1)} %all-gather.7.cloned.1.call-done) | copy-start | bytes 12582916
  118.6 22.0 %all-to-all-start.2 = ((bf16[192,4,1024]{2,0,1:T(8,128)(2,1)}), bf16[192,4,1024]{2,0,1:T(8,128)(2,1)S(1)}, u32[]{:S(2)}, u32[]{:S(2)}) async-start(bf16[192,4,1024]{2,0,1:T(8,128)(2,1)} %copy.14), calls=%async_computation.3 | async-start | bytes 3145728 | tf_op jit(solution)/shard_map/all_to_all | solution.py:71
  123.3 23.7 %copy-start.2 = (bf16[1,192,512]{2,1,0:T(8,128)(2,1)S(1)}, bf16[1,192,512]{2,1,0:T(8,128)(2,1)}, u32[]{:S(2)}) copy-start(bf16[1,192,512]{2,1,0:T(8,128)(2,1)} %get-tuple-element.18) | copy-start | bytes 589828
  125.1 22.8 %copy-start.5 = (bf16[1,2,192,512]{3,2,1,0:T(8,128)(2,1)S(1)}, bf16[1,2,192,512]{3,2,1,0:T(8,128)(2,1)}, u32[]{:S(2)}) copy-start(bf16[1,2,192,512]{3,2,1,0:T(8,128)(2,1)} %copy-done.4) | copy-start | bytes 1179652
  141.5 13.5 %all-to-all-start.1 = ((bf16[4,192,512]{2,1,0:T(8,128)(2,1)}), bf16[4,192,512]{2,1,0:T(8,128)(2,1)S(1)}, u32[]{:S(2)}, u32[]{:S(2)}) async-start(bf16[4,192,512]{2,1,0:T(8,128)(2,1)} %broadcast_in_dim.47), calls=%async_computation.2 | async-start | bytes 1572864 | tf_op jit(solution)/shard_map/all_to_all | solution.py:15
  147.9 3.8 %copy-start.3 = (bf16[1,192,512]{2,1,0:T(8,128)(2,1)S(1)}, bf16[1,192,512]{2,1,0:T(8,128)(2,1)}, u32[]{:S(2)}) copy-start(bf16[1,192,512]{2,1,0:T(8,128)(2,1)} %get-tuple-element.21) | copy-start | bytes 589828
  156.1 11.6 %copy-start.1 = (bf16[1,192,512]{2,1,0:T(8,128)(2,1)S(1)}, bf16[1,192,512]{2,1,0:T(8,128)(2,1)}, u32[]{:S(2)}) copy-start(bf16[1,192,512]{2,1,0:T(8,128)(2,1)} %bitcast_select_fusion) | copy-start | bytes 589828
Sparse Core Ops, SparseCore 0:
  10.1 56.3 all-gather.6
  79.6 38.7 all-gather.4
  121.2 45.2 reduce-scatter.1
where the time goes:
time: 175 us
  waiting for transfers between devices  99.2 us (57%)
  starting transfers between devices  34.4 us (20%)
  between operations  14.5 us (8%)
  matrix products  11 us (6%)
  local copies, waits for them, and re-layouts  10.5 us (6%)
  other arithmetic  5.23 us (3%)
    ppermute x3, waiting for transfers between devices, shifted(): return lax.ppermute(block, axis, route)  44.9 us
    all_to_all x2, waiting for transfers between devices, sent_to_all(): return lax.all_to_all(copies, axis, split_axis=0, concat_axis=0, tiled=True)  28.9 us
    ppermute x3, starting transfers between devices, shifted(): return lax.ppermute(block, axis, route)  17.7 us
    all_to_all x1, waiting for transfers between devices, local(): lax.all_to_all(lower_full, 'dp', split_axis=1, concat_axis=0, tiled=True)  15.5 us
    all_to_all x2, starting transfers between devices, sent_to_all(): return lax.all_to_all(copies, axis, split_axis=0, concat_axis=0, tiled=True)  11.9 us
    reduce_scatter x1, waiting for transfers between devices, local(): lax.psum_scatter(terms.astype(jnp.bfloat16), 'tensor', scatter_dimension=...  9.09 us
    all_to_all x1, starting transfers between devices, local(): lax.all_to_all(lower_full, 'dp', split_axis=1, concat_axis=0, tiled=True)  4.77 us
    dot_general x1, matrix products, local(): pre = jnp.dot(upper_full, whole_weight, preferred_element_type=jnp.float32)  3.74 us
  transfers between devices with their start and end apart: 9, of which 6 were waited for; matrix products, arithmetic and copies ran while one was open for 13% of the time, Pallas kernels for 0%

commit v1 on v0

v1 whole, which is shorter than its diff:
```python
import jax
import jax.numpy as jnp
from jax import lax
from jax.experimental import pallas as pl
from jax.experimental.pallas import tpu as pltpu
from jax.sharding import PartitionSpec as P


F32 = jnp.float32
BF16 = jnp.bfloat16


def shifted(block, axis, distance):
    devices = range(lax.axis_size(axis))
    route = [((i - distance) % len(devices), i) for i in devices]
    return lax.ppermute(block, axis, route)


def exchanged(block, flip):
    return lax.ppermute(block, "tensor", [(i, i ^ flip) for i in range(lax.axis_size("tensor"))])


def nn(left, right):
    return lax.dot_general(left, right, (((1,), (0,)), ((), ())), preferred_element_type=F32)


def nt(left, right):
    return lax.dot_general(left, right, (((1,), (1,)), ((), ())), preferred_element_type=F32)


def tn(left, right):
    return lax.dot_general(left, right, (((0,), (0,)), ((), ())), preferred_element_type=F32)


def places():
    along = lax.axis_index("tensor")
    return lax.axis_index("dp"), lax.div(along, 2), lax.rem(along, 2)


def shards(own, prev, nxt, far_lo, far_hi):
    half = own.shape[0] // 2
    return (
        (0, own[:half], own[half:]),
        (3, prev[:half], prev[half:]),
        (1, nxt[:half], nxt[half:]),
        (2, far_lo[...], far_hi[...]),
    )


def by_parity(core, mine, other):
    first = core == 0
    return jnp.where(first, mine, other), jnp.where(first, other, mine)


def slot(chip, k):
    e = lax.bitwise_xor(chip, k)
    return lax.rem(e, 2), lax.div(e, 2)


def picked(own_pair, near_pair, chip, k):
    which, at = slot(chip, k)
    return jnp.where(which == 0, own_pair[at], near_pair[at])


def project(mine, other, parts):
    place, chip, core = places()
    total = None
    for distance, low, high in parts:
        k = lax.rem(place + distance, 4)
        even, odd = by_parity(core, picked(*mine, chip, k), picked(*other, chip, k))
        term = nn(even, low) + nn(odd, high)
        total = term if total is None else total + term
    return total


def held_kernel(
    length, mine_a, mine_b, other_a, other_b, own, prev, nxt, far_lo, far_hi, grad, pre_out, keep_out, send_out, dp_out
):
    place, chip, core = places()
    parts = shards(own, prev, nxt, far_lo, far_hi)
    pre = project((mine_a, mine_b), (other_a, other_b), parts)
    pre_out[...] = pre
    sigma = jax.nn.sigmoid(pre)
    live = lax.broadcasted_iota(jnp.int32, pre.shape, 0) < length[0, 0]
    dupper = jnp.where(live, grad[0, 0].astype(F32), 0.0)
    hidden = (dupper * (sigma * (1.0 + pre * (1.0 - sigma)))).astype(BF16)
    for k in range(4):
        dp_out[k, 0] = picked(mine_a, mine_b, chip, k)
        dp_out[k, 1] = hidden
    for distance, low, high in parts:
        k = lax.rem(place + distance, 4)
        even = nt(hidden, low).astype(BF16)
        odd = nt(hidden, high).astype(BF16)
        which, at = slot(chip, k)
        keep, send = by_parity(core, even, odd)
        keep_out[which, at] = keep
        send_out[which, at] = send


def new_kernel(mine_a, mine_b, other_a, other_b, own, prev, nxt, far_lo, far_hi, inbound, out):
    pre = project((mine_a, mine_b), (other_a, other_b), shards(own, prev, nxt, far_lo, far_hi))
    out[0, 0] = (inbound[0, 1].astype(F32) + pre * jax.nn.sigmoid(pre)).astype(BF16)
    out[0, 1] = inbound[0, 0]


def rebuilt_kernel(pre, back, out):
    t = pre[...]
    out[0, 0] = back[0, 1]
    out[0, 1] = (back[0, 0].astype(F32) - t * jax.nn.sigmoid(t)).astype(BF16)


def grad_kernel(exchange, other, out):
    _, _, core = places()
    half = out.shape[1] // 2
    hidden = exchange[:, 1].reshape(-1, exchange.shape[-1])
    even, odd = by_parity(core, exchange[:, 0], other[...])
    out[0, :half] = tn(even.reshape(-1, half), hidden).astype(BF16)
    out[0, half:] = tn(odd.reshape(-1, half), hidden).astype(BF16)


def near_kernel(keep, received, out):
    out[...] = (keep[1].astype(F32) + received[1].astype(F32)).astype(BF16)


def far_kernel(keep, received, near, out):
    out[...] = (keep[0, 1].astype(F32) + received[0, 1].astype(F32) + near[1].astype(F32)).astype(BF16)


def last_kernel(length, keep, received, near, far, grad, out):
    live = lax.broadcasted_iota(jnp.int32, far.shape, 0) < length[0, 0]
    through = keep[0, 0].astype(F32) + received[0, 0].astype(F32) + near[0].astype(F32) + far[...].astype(F32)
    out[0, 0] = (jnp.where(live, grad[0, 1].astype(F32), 0.0) + through).astype(BF16)
    out[0, 1] = jnp.where(live, grad[0, 0].astype(F32), 0.0).astype(BF16)


def run(kernel, outs, args, flops=0, scalars=0, mib=8):
    vmem = pl.BlockSpec(memory_space=pltpu.VMEM)
    smem = pl.BlockSpec(memory_space=pltpu.SMEM)
    moved = sum(a.size * a.dtype.itemsize for a in args)
    return pl.pallas_call(
        kernel,
        out_shape=outs,
        in_specs=[smem] * scalars + [vmem] * (len(args) - scalars),
        out_specs=jax.tree.map(lambda _: vmem, outs),
        cost_estimate=pl.CostEstimate(flops=flops, transcendentals=0, bytes_accessed=moved),
        compiler_params=pltpu.CompilerParams(vmem_limit_bytes=mib * 2**20),
    )(*args)


def gathered(block):
    far = exchanged(block, 4)
    own_pair = jnp.stack([block, far])
    near_pair = exchanged(own_pair, 2)
    other_own = exchanged(own_pair, 1)
    other_near = exchanged(near_pair, 1)
    return own_pair, near_pair, other_own, other_near


def local(sent_out, sent_back, sent_grad, lengths, weight):
    tokens, width = sent_out.shape[2:]
    own = weight[0]
    depth = own.shape[0]
    half = depth // 2
    shape = jax.ShapeDtypeStruct
    pair = shape((1, 2, tokens, width), BF16)
    product = 2 * tokens * width * 4 * depth

    prev = shifted(own, "dp", 1)
    nxt = shifted(own, "dp", -1)
    back = shifted(sent_back, "section", -1)
    inbound = shifted(sent_out, "section", 1)
    grad = shifted(sent_grad, "section", -1)
    far_lo = shifted(prev[:half], "dp", 1)
    far_hi = shifted(nxt[half:], "dp", -1)
    weights = (own, prev, nxt, far_lo, far_hi)
    held = gathered(back[0, 1])
    new = gathered(inbound[0, 0])

    terms = shape((2, 2, tokens, width), BF16)
    pre_held, keep, send, share = run(
        held_kernel,
        (shape((tokens, width), F32), terms, terms, shape((4, 2, tokens, width), BF16)),
        (lengths, *held, *weights, grad),
        flops=2 * product,
        scalars=1,
        mib=20,
    )
    received = exchanged(send, 1)
    exchange = lax.all_to_all(share, "dp", 0, 0, tiled=True)
    near_sum = run(near_kernel, shape((2, tokens, width), BF16), (keep, received))
    near = exchanged(near_sum, 2)
    emitted = run(new_kernel, pair, (*new, *weights, inbound), flops=product, mib=16)
    far_sum = run(far_kernel, shape((tokens, width), BF16), (keep, received, near))
    far = exchanged(far_sum, 4)
    rebuilt = run(rebuilt_kernel, pair, (pre_held, back), flops=tokens * width)
    other = exchanged(exchange[:, 0], 1)
    weight_grad = run(grad_kernel, shape(weight.shape, BF16), (exchange, other), flops=product, mib=16)
    input_grad = run(last_kernel, pair, (lengths, keep, received, near, far, grad), scalars=1)
    return emitted, rebuilt, input_grad, weight_grad


def solution(mesh):
    act = P("section", None, "dp", "tensor")
    mat = P("section", "dp", "tensor")
    return jax.shard_map(
        local,
        mesh=mesh,
        in_specs=(act, act, act, P("section", "dp"), mat),
        out_specs=(act, act, act, mat),
        check_vma=False,
    )
```

time: 175 us -> 161 us (0.920)
  starting transfers between devices: 34.4 us -> 79.3 us
  waiting for transfers between devices: 99.2 us -> 64.9 us
  between operations: 14.5 us -> 1.79 us
  matrix products: 11 us -> 0 us
  Pallas kernels: 0 us -> 9.35 us
  local copies, waits for them, and re-layouts: 10.5 us -> 3.8 us
  other arithmetic: 5.23 us -> 0.82 us
    all_to_all x3 -> x1, waiting for transfers between devices: 44.4 us -> 0.01 us  [local(): exchange = lax.all_to_all(share, 'dp', 0, 0, tiled=True)]
    ppermute x0 -> x12, starting transfers between devices: none -> 33.3 us  [exchanged(): lax.ppermute(block, 'tensor', [(i, i ^ flip) for i in range(lax.axis_size...]
    ppermute x0 -> x12, waiting for transfers between devices: none -> 25.9 us  [exchanged(): lax.ppermute(block, 'tensor', [(i, i ^ flip) for i in range(lax.axis_size...]
    ppermute x3 -> x7, starting transfers between devices: 17.7 us -> 40.9 us  [shifted(): return lax.ppermute(block, axis, route)]
    all_to_all x3 -> x1, starting transfers between devices: 16.7 us -> 5.15 us  [local(): exchange = lax.all_to_all(share, 'dp', 0, 0, tiled=True)]
    dot_general x4 -> x0, matrix products: 11 us -> none  [the longest x1 3.74 us: local(): pre = jnp.dot(upper_full, whole_weight, preferred_element_type=jnp.float32)]
    pallas_call x0 -> x7, Pallas kernels: none -> 9.35 us  [run(): pl.pallas_call(kernel, out_shape=outs, in_specs=[smem] * scalars + [vmem]...]
    reduce_scatter x1 -> x0, waiting for transfers between devices: 9.09 us -> none  [local(): lax.psum_scatter(terms.astype(jnp.bfloat16), 'tensor', scatter_dimension=...]
  transfers between devices with their start and end apart: 9 -> 20, of which waited for: 6 -> 7; matrix products, arithmetic and copies ran while one was open for 13% -> 1% of each run, Pallas kernels for 0% -> 3%
where the time goes in v1:
time: 161 us; the launch traced here: 160 us
  starting transfers between devices  79.3 us (49%)
  waiting for transfers between devices  64.9 us (40%)
  Pallas kernels  9.35 us (6%)
  local copies, waits for them, and re-layouts  3.8 us (2%)
  between operations  1.79 us (1%)
    ppermute x7, starting transfers between devices, shifted(): return lax.ppermute(block, axis, route)  40.9 us
    ppermute x7, waiting for transfers between devices, shifted(): return lax.ppermute(block, axis, route)  39 us
    ppermute x12, starting transfers between devices, exchanged(): lax.ppermute(block, 'tensor', [(i, i ^ flip) for i in range(lax.axis_size...  33.3 us
    ppermute x12, waiting for transfers between devices, exchanged(): lax.ppermute(block, 'tensor', [(i, i ^ flip) for i in range(lax.axis_size...  25.9 us
    pallas_call x7, Pallas kernels, run(): pl.pallas_call(kernel, out_shape=outs, in_specs=[smem] * scalars + [vmem]...  9.35 us
    all_to_all x1, starting transfers between devices, local(): exchange = lax.all_to_all(share, 'dp', 0, 0, tiled=True)  5.15 us
    unnamed x38, local copies, waits for them, and re-layouts  3.62 us
  transfers between devices with their start and end apart: 20, of which 7 were waited for; matrix products, arithmetic and copies ran while one was open for 1% of the time, Pallas kernels for 3%

profile of v1, /device:TPU:6, one launch (start us, length us, event | category | flops | bytes accessed | tf_op | source)
XLA Modules:
  0.0 160.0 jit_solution(12212605678420325978)
XLA Ops:
  0.6 13.8 %collective-permute-start.9 = (bf16[1,2,192,512]{3,2,1,0:T(8,128)(2,1)}, bf16[1,2,192,512]{3,2,1,0:T(8,128)(2,1)S(1)}, u32[]{:S(2)}, u32[]{:S(2)}) collective-permute-start(bf16[1,2,192,512]{3,2,1,0:T(8,128)(2,1)} %param.6), channel_id=1, source_target_pairs={{32,0},{64,32},{96,64},{128,96},{160,128},{192,160},{224,192},{256... | collective-permute-start | bytes 1179656 | tf_op jit(solution)/shard_map/ppermute | solution.py:16
  14.5 2.4 %collective-permute-start.5 = (bf16[1024,512]{1,0:T(8,128)(2,1)}, bf16[1024,512]{1,0:T(8,128)(2,1)S(1)}, u32[]{:S(2)}, u32[]{:S(2)}) collective-permute-start(bf16[1024,512]{1,0:T(8,128)(2,1)} %bitcast.15), channel_id=1, source_target_pairs={{24,0},{0,8},{8,16},{16,24},{25,1},{1,9},{9,17},{17,25},{26,2},{2,... | collective-permute-start | bytes 3145736 | tf_op jit(solution)/shard_map/ppermute | solution.py:16
  16.9 3.5 %collective-permute-start.6 = (bf16[1024,512]{1,0:T(8,128)(2,1)}, bf16[1024,512]{1,0:T(8,128)(2,1)S(1)}, u32[]{:S(2)}, u32[]{:S(2)}) collective-permute-start(bf16[1024,512]{1,0:T(8,128)(2,1)} %bitcast.16), channel_id=1, source_target_pairs={{8,0},{16,8},{24,16},{0,24},{9,1},{17,9},{25,17},{1,25},{10,2},{18... | collective-permute-start | bytes 3145736 | tf_op jit(solution)/shard_map/ppermute | solution.py:16
  20.3 8.7 %collective-permute-done.9.back = bf16[1,2,192,512]{3,2,1,0:T(8,128)(2,1)S(1)} collective-permute-done((bf16[1,2,192,512]{3,2,1,0:T(8,128)(2,1)}, bf16[1,2,192,512]{3,2,1,0:T(8,128)(2,1)S(1)}, u32[]{:S(2)}, u32[]{:S(2)}) %collective-permute-start.9) | collective-permute-done | bytes 393248 | tf_op jit(solution)/shard_map/ppermute | solution.py:16
  29.0 0.0 copy-start.18
  29.1 0.0 copy-start.4
  29.1 3.9 %collective-permute-start.10 = (bf16[192,512]{1,0:T(8,128)(2,1)S(1)}, bf16[192,512]{1,0:T(8,128)(2,1)S(1)}, u32[]{:S(2)}, u32[]{:S(2)}) collective-permute-start(bf16[192,512]{1,0:T(8,128)(2,1)S(1)} %get-tuple-element.13), channel_id=1, source_target_pairs={{0,4},{1,5},{2,6},{3,7},{4,0},{5,1},{6,2},{7,3},{8,12},{9,13},{10,... | collective-permute-start | bytes 589832 | tf_op jit(solution)/shard_map/ppermute | solution.py:20
  33.0 8.2 %collective-permute-done.10 = bf16[192,512]{1,0:T(8,128)(2,1)S(1)} collective-permute-done((bf16[192,512]{1,0:T(8,128)(2,1)S(1)}, bf16[192,512]{1,0:T(8,128)(2,1)S(1)}, u32[]{:S(2)}, u32[]{:S(2)}) %collective-permute-start.10) | collective-permute-done | bytes 196640 | tf_op jit(solution)/shard_map/ppermute | solution.py:20
  41.3 1.9 %collective-permute-start.11 = (bf16[2,192,512]{2,1,0:T(8,128)(2,1)S(1)}, bf16[2,192,512]{2,1,0:T(8,128)(2,1)S(1)}, u32[]{:S(2)}, u32[]{:S(2)}) collective-permute-start(bf16[2,192,512]{2,1,0:T(8,128)(2,1)S(1)} %pad_maximum_fusion.1.mine_a), channel_id=1, source_target_pairs={{0,2},{1,3},{2,0},{3,1},{4,6},{5,7},{6,4},{7,5},{8,10},{9,11},{10,... | collective-permute-start | bytes 1179656 | tf_op jit(solution)/shard_map/ppermute | solution.py:20
  43.2 0.0 copy-start
  43.3 2.4 %collective-permute-start.7 = (bf16[512,512]{1,0:T(8,128)(2,1)S(1)}, bf16[512,512]{1,0:T(8,128)(2,1)S(1)}, u32[]{:S(2)}, u32[]{:S(2)}) collective-permute-start(bf16[512,512]{1,0:T(8,128)(2,1)S(1)} %slice.21), channel_id=1, source_target_pairs={{24,0},{0,8},{8,16},{16,24},{25,1},{1,9},{9,17},{17,25},{26,2},{2,... | collective-permute-start | bytes 1572872 | tf_op jit(solution)/shard_map/ppermute | solution.py:16
  45.8 3.5 %collective-permute-start.8 = (bf16[512,512]{1,0:T(8,128)(2,1)S(1)}, bf16[512,512]{1,0:T(8,128)(2,1)S(1)}, u32[]{:S(2)}, u32[]{:S(2)}) collective-permute-start(bf16[512,512]{1,0:T(8,128)(2,1)S(1)} %slice.22), channel_id=1, source_target_pairs={{8,0},{16,8},{24,16},{0,24},{9,1},{17,9},{25,17},{1,25},{10,2},{18... | collective-permute-start | bytes 1572872 | tf_op jit(solution)/shard_map/ppermute | solution.py:16
  49.2 13.5 %collective-permute-start.14 = (bf16[1,2,192,512]{3,2,1,0:T(8,128)(2,1)S(1)}, bf16[1,2,192,512]{3,2,1,0:T(8,128)(2,1)S(1)}, u32[]{:S(2)}, u32[]{:S(2)}) collective-permute-start(bf16[1,2,192,512]{3,2,1,0:T(8,128)(2,1)S(1)} %copy-done.18), channel_id=1, source_target_pairs={{32,0},{64,32},{96,64},{128,96},{160,128},{192,160},{224,192},{256... | collective-permute-start | bytes 1179656 | tf_op jit(solution)/shard_map/ppermute | solution.py:16
  62.7 1.9 %collective-permute-start.12 = (bf16[2,192,512]{2,1,0:T(8,128)(2,1)S(1)}, bf16[2,192,512]{2,1,0:T(8,128)(2,1)S(1)}, u32[]{:S(2)}, u32[]{:S(2)}) collective-permute-start(bf16[2,192,512]{2,1,0:T(8,128)(2,1)S(1)} %pad_maximum_fusion.1.mine_a), channel_id=1, source_target_pairs={{0,1},{1,0},{2,3},{3,2},{4,5},{5,4},{6,7},{7,6},{8,9},{9,8},{10,11... | collective-permute-start | bytes 1179656 | tf_op jit(solution)/shard_map/ppermute | solution.py:20
  64.6 2.4 %collective-permute-start.13 = (bf16[2,192,512]{2,1,0:T(8,128)(2,1)S(1)}, bf16[2,192,512]{2,1,0:T(8,128)(2,1)S(1)}, u32[]{:S(2)}, u32[]{:S(2)}) collective-permute-start(bf16[2,192,512]{2,1,0:T(8,128)(2,1)S(1)} %collective-permute-done.11.mine_b), channel_id=1, source_target_pairs={{0,1},{1,0},{2,3},{3,2},{4,5},{5,4},{6,7},{7,6},{8,9},{9,8},{10,11... | collective-permute-start | bytes 1179656 | tf_op jit(solution)/shard_map/ppermute | solution.py:20
  67.7 8.0 %collective-permute-done.14.grad = bf16[1,2,192,512]{3,2,1,0:T(8,128)(2,1)S(1)} collective-permute-done((bf16[1,2,192,512]{3,2,1,0:T(8,128)(2,1)S(1)}, bf16[1,2,192,512]{3,2,1,0:T(8,128)(2,1)S(1)}, u32[]{:S(2)}, u32[]{:S(2)}) %collective-permute-start.14) | collective-permute-done | bytes 393248 | tf_op jit(solution)/shard_map/ppermute | solution.py:16
  75.7 2.5 %shard_map.85 = (f32[192,512]{1,0:T(8,128)S(1)}, bf16[2,2,192,512]{3,2,1,0:T(8,128)(2,1)S(1)}, bf16[2,2,192,512]{3,2,1,0:T(8,128)(2,1)S(1)}, bf16[4,2,192,512]{3,2,1,0:T(8,128)(2,1)S(1)}) custom-call(s32[1,1]{1,0:T(1,128)S(6)} %copy.13.length, bf16[2,192,512]{2,1,0:T(8,128)(2,1)S(1)} %pad_maximum_fusion.1.mine_a, ...), custom_call_target="tpu_custom_call" | custom-call | flops 1610612736 | bytes 6160388 | tf_op jit(solution)/shard_map/pallas_call | solution.py:140
  78.3 1.2 copy-done.10
  79.5 0.7 copy-done.15
  80.2 0.9 copy-done.17
  81.1 5.1 %all-to-all-start = ((bf16[4,2,192,512]{3,2,1,0:T(8,128)(2,1)}), bf16[4,2,192,512]{3,2,1,0:T(8,128)(2,1)S(1)}, u32[]{:S(2)}, u32[]{:S(2)}) async-start(bf16[4,2,192,512]{3,2,1,0:T(8,128)(2,1)} %copy-done.10), calls=%async_computation | async-start | bytes 3145728 | tf_op jit(solution)/shard_map/all_to_all | solution.py:189
  86.3 1.9 %collective-permute-start = (bf16[1,2,192,512]{3,2,1,0:T(8,128)(2,1)}, bf16[1,2,192,512]{3,2,1,0:T(8,128)(2,1)S(1)}, u32[]{:S(2)}, u32[]{:S(2)}) collective-permute-start(bf16[1,2,192,512]{3,2,1,0:T(8,128)(2,1)} %param.5), channel_id=1, source_target_pairs={{480,0},{0,32},{32,64},{64,96},{96,128},{128,160},{160,192},{192,2... | collective-permute-start | bytes 1179656 | tf_op jit(solution)/shard_map/ppermute | solution.py:16
  88.2 1.9 %collective-permute-start.15 = (bf16[2,2,192,512]{3,2,1,0:T(8,128)(2,1)}, bf16[2,2,192,512]{3,2,1,0:T(8,128)(2,1)S(1)}, u32[]{:S(2)}, u32[]{:S(2)}) collective-permute-start(bf16[2,2,192,512]{3,2,1,0:T(8,128)(2,1)} %copy-done.17), channel_id=1, source_target_pairs={{0,1},{1,0},{2,3},{3,2},{4,5},{5,4},{6,7},{7,6},{8,9},{9,8},{10,11... | collective-permute-start | bytes 2359304 | tf_op jit(solution)/shard_map/ppermute | solution.py:20
  90.1 22.4 %collective-permute-done.inbound = bf16[1,2,192,512]{3,2,1,0:T(8,128)(2,1)S(1)} collective-permute-done((bf16[1,2,192,512]{3,2,1,0:T(8,128)(2,1)}, bf16[1,2,192,512]{3,2,1,0:T(8,128)(2,1)S(1)}, u32[]{:S(2)}, u32[]{:S(2)}) %collective-permute-start) | collective-permute-done | bytes 393248 | tf_op jit(solution)/shard_map/ppermute | solution.py:16
  112.5 0.0 copy-start.11
  112.5 0.7 copy-done.11
  113.3 4.0 %collective-permute-start.1 = (bf16[192,512]{1,0:T(8,128)(2,1)S(1)}, bf16[192,512]{1,0:T(8,128)(2,1)S(1)}, u32[]{:S(2)}, u32[]{:S(2)}) collective-permute-start(bf16[192,512]{1,0:T(8,128)(2,1)S(1)} %get-tuple-element.15), channel_id=1, source_target_pairs={{0,4},{1,5},{2,6},{3,7},{4,0},{5,1},{6,2},{7,3},{8,12},{9,13},{10,... | collective-permute-start | bytes 589832 | tf_op jit(solution)/shard_map/ppermute | solution.py:20
  117.3 6.3 %collective-permute-done.1 = bf16[192,512]{1,0:T(8,128)(2,1)S(1)} collective-permute-done((bf16[192,512]{1,0:T(8,128)(2,1)S(1)}, bf16[192,512]{1,0:T(8,128)(2,1)S(1)}, u32[]{:S(2)}, u32[]{:S(2)}) %collective-permute-start.1) | collective-permute-done | bytes 196640 | tf_op jit(solution)/shard_map/ppermute | solution.py:20
  123.6 0.8 pad_maximum_fusion.mine_a
  124.3 3.0 %collective-permute-start.2 = (bf16[2,192,512]{2,1,0:T(8,128)(2,1)}, bf16[2,192,512]{2,1,0:T(8,128)(2,1)}, u32[]{:S(2)}, u32[]{:S(2)}) collective-permute-start(bf16[2,192,512]{2,1,0:T(8,128)(2,1)} %pad_maximum_fusion.mine_a), channel_id=1, source_target_pairs={{0,2},{1,3},{2,0},{3,1},{4,6},{5,7},{6,4},{7,5},{8,10},{9,11},{10,... | collective-permute-start | bytes 1179656 | tf_op jit(solution)/shard_map/ppermute | solution.py:20
  127.3 0.0 copy-start.16
  127.4 0.1 slice_bitcast_fusion
  127.4 2.1 %collective-permute-start.18 = (bf16[4,192,512]{2,1,0:T(8,128)(2,1)S(1)}, bf16[4,192,512]{2,1,0:T(8,128)(2,1)S(1)}, u32[]{:S(2)}, u32[]{:S(2)}) collective-permute-start(bf16[4,192,512]{2,1,0:T(8,128)(2,1)S(1)} %slice_bitcast_fusion), channel_id=1, source_target_pairs={{0,1},{1,0},{2,3},{3,2},{4,5},{5,4},{6,7},{7,6},{8,9},{9,8},{10,11... | collective-permute-start | bytes 2359304 | tf_op jit(solution)/shard_map/ppermute | solution.py:20
  129.5 0.0 copy-start.12
  129.5 0.1 shard_map.87
  129.6 0.0 copy-start.1
  129.7 0.0 copy-start.5
  129.7 3.1 %collective-permute-start.16 = (bf16[2,192,512]{2,1,0:T(8,128)(2,1)S(1)}, bf16[2,192,512]{2,1,0:T(8,128)(2,1)S(1)}, u32[]{:S(2)}, u32[]{:S(2)}) collective-permute-start(bf16[2,192,512]{2,1,0:T(8,128)(2,1)S(1)} %shard_map.87), channel_id=1, source_target_pairs={{0,2},{1,3},{2,0},{3,1},{4,6},{5,7},{6,4},{7,5},{8,10},{9,11},{10,... | collective-permute-start | bytes 1179656 | tf_op jit(solution)/shard_map/ppermute | solution.py:20
  132.8 2.1 %collective-permute-start.3 = (bf16[2,192,512]{2,1,0:T(8,128)(2,1)}, bf16[2,192,512]{2,1,0:T(8,128)(2,1)S(1)}, u32[]{:S(2)}, u32[]{:S(2)}) collective-permute-start(bf16[2,192,512]{2,1,0:T(8,128)(2,1)} %pad_maximum_fusion.mine_a), channel_id=1, source_target_pairs={{0,1},{1,0},{2,3},{3,2},{4,5},{5,4},{6,7},{7,6},{8,9},{9,8},{10,11... | collective-permute-start | bytes 1179656 | tf_op jit(solution)/shard_map/ppermute | solution.py:20
  134.9 2.2 %collective-permute-start.4 = (bf16[2,192,512]{2,1,0:T(8,128)(2,1)}, bf16[2,192,512]{2,1,0:T(8,128)(2,1)S(1)}, u32[]{:S(2)}, u32[]{:S(2)}) collective-permute-start(bf16[2,192,512]{2,1,0:T(8,128)(2,1)} %collective-permute-done.2.mine_b), channel_id=1, source_target_pairs={{0,1},{1,0},{2,3},{3,2},{4,5},{5,4},{6,7},{7,6},{8,9},{9,8},{10,11... | collective-permute-start | bytes 1179656 | tf_op jit(solution)/shard_map/ppermute | solution.py:20
  137.1 6.2 %collective-permute-done.16.near = bf16[2,192,512]{2,1,0:T(8,128)(2,1)S(1)} collective-permute-done((bf16[2,192,512]{2,1,0:T(8,128)(2,1)S(1)}, bf16[2,192,512]{2,1,0:T(8,128)(2,1)S(1)}, u32[]{:S(2)}, u32[]{:S(2)}) %collective-permute-start.16) | collective-permute-done | bytes 393248 | tf_op jit(solution)/shard_map/ppermute | solution.py:20
  143.3 0.1 shard_map.88
  143.4 4.8 %collective-permute-start.17 = (bf16[192,512]{1,0:T(8,128)(2,1)S(1)}, bf16[192,512]{1,0:T(8,128)(2,1)S(1)}, u32[]{:S(2)}, u32[]{:S(2)}) collective-permute-start(bf16[192,512]{1,0:T(8,128)(2,1)S(1)} %shard_map.88), channel_id=1, source_target_pairs={{0,4},{1,5},{2,6},{3,7},{4,0},{5,1},{6,2},{7,3},{8,12},{9,13},{10,... | collective-permute-start | bytes 589832 | tf_op jit(solution)/shard_map/ppermute | solution.py:20
  148.2 0.8 shard_map.86
  149.1 2.9 %shard_map.84 = bf16[1,2,192,512]{3,2,1,0:T(8,128)(2,1)} custom-call(bf16[2,192,512]{2,1,0:T(8,128)(2,1)} %pad_maximum_fusion.mine_a, bf16[2,192,512]{2,1,0:T(8,128)(2,1)} %collective-permute-done.2.mine_b, bf16[2,192,512]{2,1,0:T(8,128)(2,1)S(1)} %collective-permute-done.3.other_a, bf16[2,192,512]{2,1,0:T(8,128)(2,1)S(1)} %collective-permute-done.4.other_b, ...), custom_call_target="tpu_custom_call" | custom-call | flops 805306368 | bytes 6160384 | tf_op jit(solution)/shard_map/pallas_call | solution.py:140
  152.0 5.1 %collective-permute-done.17.far = bf16[192,512]{1,0:T(8,128)(2,1)S(1)} collective-permute-done((bf16[192,512]{1,0:T(8,128)(2,1)S(1)}, bf16[192,512]{1,0:T(8,128)(2,1)S(1)}, u32[]{:S(2)}, u32[]{:S(2)}) %collective-permute-start.17) | collective-permute-done | bytes 196640 | tf_op jit(solution)/shard_map/ppermute | solution.py:20
  157.1 0.9 shard_map.89
  158.0 2.0 %shard_map.90 = bf16[1,1024,512]{2,1,0:T(8,128)(2,1)} custom-call(bf16[4,2,192,512]{3,2,1,0:T(8,128)(2,1)S(1)} %all-to-all-done.exchange, bf16[4,192,512]{2,1,0:T(8,128)(2,1)S(1)} %collective-permute-done.18.other), custom_call_target="tpu_custom_call" | custom-call | flops 805306368 | bytes 2359296 | tf_op jit(solution)/shard_map/pallas_call | solution.py:140
  (44 shorter events, 0.2 us)
Async XLA Ops:
  0.6 28.4 %collective-permute-start.9 = (bf16[1,2,192,512]{3,2,1,0:T(8,128)(2,1)}, bf16[1,2,192,512]{3,2,1,0:T(8,128)(2,1)S(1)}, u32[]{:S(2)}, u32[]{:S(2)}) collective-permute-start(bf16[1,2,192,512]{3,2,1,0:T(8,128)(2,1)} %param.6), channel_id=1, source_target_pairs={{32,0},{64,32},{96,64},{128,96},{160,128},{192,160},{224,192},{256... | collective-permute-start | bytes 1179656 | tf_op jit(solution)/shard_map/ppermute | solution.py:16
  14.5 28.8 %collective-permute-start.5 = (bf16[1024,512]{1,0:T(8,128)(2,1)}, bf16[1024,512]{1,0:T(8,128)(2,1)S(1)}, u32[]{:S(2)}, u32[]{:S(2)}) collective-permute-start(bf16[1024,512]{1,0:T(8,128)(2,1)} %bitcast.15), channel_id=1, source_target_pairs={{24,0},{0,8},{8,16},{16,24},{25,1},{1,9},{9,17},{17,25},{26,2},{2,... | collective-permute-start | bytes 3145736 | tf_op jit(solution)/shard_map/ppermute | solution.py:16
  16.9 28.8 %collective-permute-start.6 = (bf16[1024,512]{1,0:T(8,128)(2,1)}, bf16[1024,512]{1,0:T(8,128)(2,1)S(1)}, u32[]{:S(2)}, u32[]{:S(2)}) collective-permute-start(bf16[1024,512]{1,0:T(8,128)(2,1)} %bitcast.16), channel_id=1, source_target_pairs={{8,0},{16,8},{24,16},{0,24},{9,1},{17,9},{25,17},{1,25},{10,2},{18... | collective-permute-start | bytes 3145736 | tf_op jit(solution)/shard_map/ppermute | solution.py:16
  29.0 16.7 %copy-start.13 = (bf16[1,2,192,512]{3,2,1,0:T(8,128)(2,1)}, bf16[1,2,192,512]{3,2,1,0:T(8,128)(2,1)S(1)}, u32[]{:S(2)}) copy-start(bf16[1,2,192,512]{3,2,1,0:T(8,128)(2,1)S(1)} %collective-permute-done.9.back) | copy-start | bytes 1179652
  29.0 20.2 %copy-start.18 = (bf16[1,2,192,512]{3,2,1,0:T(8,128)(2,1)S(1)}, bf16[1,2,192,512]{3,2,1,0:T(8,128)(2,1)}, u32[]{:S(2)}) copy-start(bf16[1,2,192,512]{3,2,1,0:T(8,128)(2,1)} %param.7) | copy-start | bytes 1179652
  29.1 46.6 %copy-start.4 = (bf16[1,1024,512]{2,1,0:T(8,128)(2,1)S(1)}, bf16[1,1024,512]{2,1,0:T(8,128)(2,1)}, u32[]{:S(2)}) copy-start(bf16[1,1024,512]{2,1,0:T(8,128)(2,1)} %param.9) | copy-start | bytes 3145732
  29.1 12.2 %collective-permute-start.10 = (bf16[192,512]{1,0:T(8,128)(2,1)S(1)}, bf16[192,512]{1,0:T(8,128)(2,1)S(1)}, u32[]{:S(2)}, u32[]{:S(2)}) collective-permute-start(bf16[192,512]{1,0:T(8,128)(2,1)S(1)} %get-tuple-element.13), channel_id=1, source_target_pairs={{0,4},{1,5},{2,6},{3,7},{4,0},{5,1},{6,2},{7,3},{8,12},{9,13},{10,... | collective-permute-start | bytes 589832 | tf_op jit(solution)/shard_map/ppermute | solution.py:20
  41.3 23.3 %collective-permute-start.11 = (bf16[2,192,512]{2,1,0:T(8,128)(2,1)S(1)}, bf16[2,192,512]{2,1,0:T(8,128)(2,1)S(1)}, u32[]{:S(2)}, u32[]{:S(2)}) collective-permute-start(bf16[2,192,512]{2,1,0:T(8,128)(2,1)S(1)} %pad_maximum_fusion.1.mine_a), channel_id=1, source_target_pairs={{0,2},{1,3},{2,0},{3,1},{4,6},{5,7},{6,4},{7,5},{8,10},{9,11},{10,... | collective-permute-start | bytes 1179656 | tf_op jit(solution)/shard_map/ppermute | solution.py:20
  43.2 35.0 %copy-start = (bf16[1024,512]{1,0:T(8,128)(2,1)}, bf16[1024,512]{1,0:T(8,128)(2,1)S(1)}, u32[]{:S(2)}) copy-start(bf16[1024,512]{1,0:T(8,128)(2,1)S(1)} %collective-permute-done.5.prev) | copy-start | bytes 3145732
  43.3 32.4 %collective-permute-start.7 = (bf16[512,512]{1,0:T(8,128)(2,1)S(1)}, bf16[512,512]{1,0:T(8,128)(2,1)S(1)}, u32[]{:S(2)}, u32[]{:S(2)}) collective-permute-start(bf16[512,512]{1,0:T(8,128)(2,1)S(1)} %slice.21), channel_id=1, source_target_pairs={{24,0},{0,8},{8,16},{16,24},{25,1},{1,9},{9,17},{17,25},{26,2},{2,... | collective-permute-start | bytes 1572872 | tf_op jit(solution)/shard_map/ppermute | solution.py:16
  45.7 32.6 %copy-start.2 = (bf16[1024,512]{1,0:T(8,128)(2,1)}, bf16[1024,512]{1,0:T(8,128)(2,1)S(1)}, u32[]{:S(2)}) copy-start(bf16[1024,512]{1,0:T(8,128)(2,1)S(1)} %collective-permute-done.6.nxt) | copy-start | bytes 3145732
  45.8 29.9 %collective-permute-start.8 = (bf16[512,512]{1,0:T(8,128)(2,1)S(1)}, bf16[512,512]{1,0:T(8,128)(2,1)S(1)}, u32[]{:S(2)}, u32[]{:S(2)}) collective-permute-start(bf16[512,512]{1,0:T(8,128)(2,1)S(1)} %slice.22), channel_id=1, source_target_pairs={{8,0},{16,8},{24,16},{0,24},{9,1},{17,9},{25,17},{1,25},{10,2},{18... | collective-permute-start | bytes 1572872 | tf_op jit(solution)/shard_map/ppermute | solution.py:16
  49.2 26.4 %collective-permute-start.14 = (bf16[1,2,192,512]{3,2,1,0:T(8,128)(2,1)S(1)}, bf16[1,2,192,512]{3,2,1,0:T(8,128)(2,1)S(1)}, u32[]{:S(2)}, u32[]{:S(2)}) collective-permute-start(bf16[1,2,192,512]{3,2,1,0:T(8,128)(2,1)S(1)} %copy-done.18), channel_id=1, source_target_pairs={{32,0},{64,32},{96,64},{128,96},{160,128},{192,160},{224,192},{256... | collective-permute-start | bytes 1179656 | tf_op jit(solution)/shard_map/ppermute | solution.py:16
  62.7 13.0 %collective-permute-start.12 = (bf16[2,192,512]{2,1,0:T(8,128)(2,1)S(1)}, bf16[2,192,512]{2,1,0:T(8,128)(2,1)S(1)}, u32[]{:S(2)}, u32[]{:S(2)}) collective-permute-start(bf16[2,192,512]{2,1,0:T(8,128)(2,1)S(1)} %pad_maximum_fusion.1.mine_a), channel_id=1, source_target_pairs={{0,1},{1,0},{2,3},{3,2},{4,5},{5,4},{6,7},{7,6},{8,9},{9,8},{10,11... | collective-permute-start | bytes 1179656 | tf_op jit(solution)/shard_map/ppermute | solution.py:20
  64.6 11.0 %collective-permute-start.13 = (bf16[2,192,512]{2,1,0:T(8,128)(2,1)S(1)}, bf16[2,192,512]{2,1,0:T(8,128)(2,1)S(1)}, u32[]{:S(2)}, u32[]{:S(2)}) collective-permute-start(bf16[2,192,512]{2,1,0:T(8,128)(2,1)S(1)} %collective-permute-done.11.mine_b), channel_id=1, source_target_pairs={{0,1},{1,0},{2,3},{3,2},{4,5},{5,4},{6,7},{7,6},{8,9},{9,8},{10,11... | collective-permute-start | bytes 1179656 | tf_op jit(solution)/shard_map/ppermute | solution.py:20
  75.7 2.6 %copy-start.6 = (bf16[512,512]{1,0:T(8,128)(2,1)}, bf16[512,512]{1,0:T(8,128)(2,1)S(1)}, u32[]{:S(2)}) copy-start(bf16[512,512]{1,0:T(8,128)(2,1)S(1)} %collective-permute-done.7.far_lo) | copy-start | bytes 1572868
  75.7 2.6 %copy-start.8 = (bf16[512,512]{1,0:T(8,128)(2,1)}, bf16[512,512]{1,0:T(8,128)(2,1)S(1)}, u32[]{:S(2)}) copy-start(bf16[512,512]{1,0:T(8,128)(2,1)S(1)} %collective-permute-done.8.far_hi) | copy-start | bytes 1572868
  78.3 1.2 copy-start.10
  79.5 0.7 copy-start.15
  80.2 0.9 copy-start.17
  81.1 46.2 %all-to-all-start = ((bf16[4,2,192,512]{3,2,1,0:T(8,128)(2,1)}), bf16[4,2,192,512]{3,2,1,0:T(8,128)(2,1)S(1)}, u32[]{:S(2)}, u32[]{:S(2)}) async-start(bf16[4,2,192,512]{3,2,1,0:T(8,128)(2,1)} %copy-done.10), calls=%async_computation | async-start | bytes 3145728 | tf_op jit(solution)/shard_map/all_to_all | solution.py:189
  86.3 26.2 %collective-permute-start = (bf16[1,2,192,512]{3,2,1,0:T(8,128)(2,1)}, bf16[1,2,192,512]{3,2,1,0:T(8,128)(2,1)S(1)}, u32[]{:S(2)}, u32[]{:S(2)}) collective-permute-start(bf16[1,2,192,512]{3,2,1,0:T(8,128)(2,1)} %param.5), channel_id=1, source_target_pairs={{480,0},{0,32},{32,64},{64,96},{96,128},{128,160},{160,192},{192,2... | collective-permute-start | bytes 1179656 | tf_op jit(solution)/shard_map/ppermute | solution.py:16
  88.2 41.3 %collective-permute-start.15 = (bf16[2,2,192,512]{3,2,1,0:T(8,128)(2,1)}, bf16[2,2,192,512]{3,2,1,0:T(8,128)(2,1)S(1)}, u32[]{:S(2)}, u32[]{:S(2)}) collective-permute-start(bf16[2,2,192,512]{3,2,1,0:T(8,128)(2,1)} %copy-done.17), channel_id=1, source_target_pairs={{0,1},{1,0},{2,3},{3,2},{4,5},{5,4},{6,7},{7,6},{8,9},{9,8},{10,11... | collective-permute-start | bytes 2359304 | tf_op jit(solution)/shard_map/ppermute | solution.py:20
  112.5 0.7 copy-start.11
  113.3 10.3 %collective-permute-start.1 = (bf16[192,512]{1,0:T(8,128)(2,1)S(1)}, bf16[192,512]{1,0:T(8,128)(2,1)S(1)}, u32[]{:S(2)}, u32[]{:S(2)}) collective-permute-start(bf16[192,512]{1,0:T(8,128)(2,1)S(1)} %get-tuple-element.15), channel_id=1, source_target_pairs={{0,4},{1,5},{2,6},{3,7},{4,0},{5,1},{6,2},{7,3},{8,12},{9,13},{10,... | collective-permute-start | bytes 589832 | tf_op jit(solution)/shard_map/ppermute | solution.py:20
  124.3 10.6 %collective-permute-start.2 = (bf16[2,192,512]{2,1,0:T(8,128)(2,1)}, bf16[2,192,512]{2,1,0:T(8,128)(2,1)}, u32[]{:S(2)}, u32[]{:S(2)}) collective-permute-start(bf16[2,192,512]{2,1,0:T(8,128)(2,1)} %pad_maximum_fusion.mine_a), channel_id=1, source_target_pairs={{0,2},{1,3},{2,0},{3,1},{4,6},{5,7},{6,4},{7,5},{8,10},{9,11},{10,... | collective-permute-start | bytes 1179656 | tf_op jit(solution)/shard_map/ppermute | solution.py:20
  127.3 20.8 %copy-start.16 = (f32[192,512]{1,0:T(8,128)S(1)}, f32[192,512]{1,0:T(8,128)}, u32[]{:S(2)}) copy-start(f32[192,512]{1,0:T(8,128)} %copy-done.15) | copy-start | bytes 1179652
  127.4 30.6 %collective-permute-start.18 = (bf16[4,192,512]{2,1,0:T(8,128)(2,1)S(1)}, bf16[4,192,512]{2,1,0:T(8,128)(2,1)S(1)}, u32[]{:S(2)}, u32[]{:S(2)}) collective-permute-start(bf16[4,192,512]{2,1,0:T(8,128)(2,1)S(1)} %slice_bitcast_fusion), channel_id=1, source_target_pairs={{0,1},{1,0},{2,3},{3,2},{4,5},{5,4},{6,7},{7,6},{8,9},{9,8},{10,11... | collective-permute-start | bytes 2359304 | tf_op jit(solution)/shard_map/ppermute | solution.py:20
  129.5 18.7 %copy-start.14 = (bf16[1,2,192,512]{3,2,1,0:T(8,128)(2,1)S(1)}, bf16[1,2,192,512]{3,2,1,0:T(8,128)(2,1)}, u32[]{:S(2)}) copy-start(bf16[1,2,192,512]{3,2,1,0:T(8,128)(2,1)} %copy-done.13) | copy-start | bytes 1179652
  129.5 19.5 %copy-start.7 = (bf16[512,512]{1,0:T(8,128)(2,1)S(1)}, bf16[512,512]{1,0:T(8,128)(2,1)}, u32[]{:S(2)}) copy-start(bf16[512,512]{1,0:T(8,128)(2,1)} %copy-done.6) | copy-start | bytes 1572868
  129.5 19.5 %copy-start.9 = (bf16[512,512]{1,0:T(8,128)(2,1)S(1)}, bf16[512,512]{1,0:T(8,128)(2,1)}, u32[]{:S(2)}) copy-start(bf16[512,512]{1,0:T(8,128)(2,1)} %copy-done.8) | copy-start | bytes 1572868
  129.5 19.5 %copy-start.12 = (bf16[1,2,192,512]{3,2,1,0:T(8,128)(2,1)S(1)}, bf16[1,2,192,512]{3,2,1,0:T(8,128)(2,1)}, u32[]{:S(2)}) copy-start(bf16[1,2,192,512]{3,2,1,0:T(8,128)(2,1)} %copy-done.11) | copy-start | bytes 1179652
  129.6 19.4 %copy-start.1 = (bf16[1024,512]{1,0:T(8,128)(2,1)S(1)}, bf16[1024,512]{1,0:T(8,128)(2,1)}, u32[]{:S(2)}) copy-start(bf16[1024,512]{1,0:T(8,128)(2,1)} %copy-done) | copy-start | bytes 3145732
  129.6 19.4 %copy-start.3 = (bf16[1024,512]{1,0:T(8,128)(2,1)S(1)}, bf16[1024,512]{1,0:T(8,128)(2,1)}, u32[]{:S(2)}) copy-start(bf16[1024,512]{1,0:T(8,128)(2,1)} %copy-done.2) | copy-start | bytes 3145732
  129.7 19.4 %copy-start.5 = (bf16[1,1024,512]{2,1,0:T(8,128)(2,1)S(1)}, bf16[1,1024,512]{2,1,0:T(8,128)(2,1)}, u32[]{:S(2)}) copy-start(bf16[1,1024,512]{2,1,0:T(8,128)(2,1)} %param.9) | copy-start | bytes 3145732
  129.7 13.7 %collective-permute-start.16 = (bf16[2,192,512]{2,1,0:T(8,128)(2,1)S(1)}, bf16[2,192,512]{2,1,0:T(8,128)(2,1)S(1)}, u32[]{:S(2)}, u32[]{:S(2)}) collective-permute-start(bf16[2,192,512]{2,1,0:T(8,128)(2,1)S(1)} %shard_map.87), channel_id=1, source_target_pairs={{0,2},{1,3},{2,0},{3,1},{4,6},{5,7},{6,4},{7,5},{8,10},{9,11},{10,... | collective-permute-start | bytes 1179656 | tf_op jit(solution)/shard_map/ppermute | solution.py:20
  132.8 16.3 %collective-permute-start.3 = (bf16[2,192,512]{2,1,0:T(8,128)(2,1)}, bf16[2,192,512]{2,1,0:T(8,128)(2,1)S(1)}, u32[]{:S(2)}, u32[]{:S(2)}) collective-permute-start(bf16[2,192,512]{2,1,0:T(8,128)(2,1)} %pad_maximum_fusion.mine_a), channel_id=1, source_target_pairs={{0,1},{1,0},{2,3},{3,2},{4,5},{5,4},{6,7},{7,6},{8,9},{9,8},{10,11... | collective-permute-start | bytes 1179656 | tf_op jit(solution)/shard_map/ppermute | solution.py:20
  134.9 14.1 %collective-permute-start.4 = (bf16[2,192,512]{2,1,0:T(8,128)(2,1)}, bf16[2,192,512]{2,1,0:T(8,128)(2,1)S(1)}, u32[]{:S(2)}, u32[]{:S(2)}) collective-permute-start(bf16[2,192,512]{2,1,0:T(8,128)(2,1)} %collective-permute-done.2.mine_b), channel_id=1, source_target_pairs={{0,1},{1,0},{2,3},{3,2},{4,5},{5,4},{6,7},{7,6},{8,9},{9,8},{10,11... | collective-permute-start | bytes 1179656 | tf_op jit(solution)/shard_map/ppermute | solution.py:20
  143.4 13.7 %collective-permute-start.17 = (bf16[192,512]{1,0:T(8,128)(2,1)S(1)}, bf16[192,512]{1,0:T(8,128)(2,1)S(1)}, u32[]{:S(2)}, u32[]{:S(2)}) collective-permute-start(bf16[192,512]{1,0:T(8,128)(2,1)S(1)} %shard_map.88), channel_id=1, source_target_pairs={{0,4},{1,5},{2,6},{3,7},{4,0},{5,1},{6,2},{7,3},{8,12},{9,13},{10,... | collective-permute-start | bytes 589832 | tf_op jit(solution)/shard_map/ppermute | solution.py:20

commit v2 on v1

--- a/solution.py
+++ b/solution.py
@@ -74,19 +74,22 @@
 
 
 def held_kernel(
-    length, mine_a, mine_b, other_a, other_b, own, prev, nxt, far_lo, far_hi, grad, pre_out, keep_out, send_out, dp_out
+    length, mine_a, mine_b, other_a, other_b, own, prev, nxt, far_lo, far_hi, grad, keep_out, send_out, own_out, dp_1, dp_2, dp_3, pre_out
 ):
     place, chip, core = places()
     parts = shards(own, prev, nxt, far_lo, far_hi)
     pre = project((mine_a, mine_b), (other_a, other_b), parts)
+    sigma = jax.nn.sigmoid(pre)
     pre_out[...] = pre
-    sigma = jax.nn.sigmoid(pre)
     live = lax.broadcasted_iota(jnp.int32, pre.shape, 0) < length[0, 0]
-    dupper = jnp.where(live, grad[0, 0].astype(F32), 0.0)
+    dupper = jnp.where(live, grad[...].astype(F32), 0.0)
     hidden = (dupper * (sigma * (1.0 + pre * (1.0 - sigma)))).astype(BF16)
-    for k in range(4):
-        dp_out[k, 0] = picked(mine_a, mine_b, chip, k)
-        dp_out[k, 1] = hidden
+    own_out[0] = picked(mine_a, mine_b, chip, place)
+    own_out[1] = picked(other_a, other_b, chip, place)
+    own_out[2] = hidden
+    for distance, out in ((1, dp_1), (2, dp_2), (3, dp_3)):
+        out[0] = picked(mine_a, mine_b, chip, lax.rem(place + distance, 4))
+        out[1] = hidden
     for distance, low, high in parts:
         k = lax.rem(place + distance, 4)
         even = nt(hidden, low).astype(BF16)
@@ -103,19 +106,39 @@
     out[0, 1] = inbound[0, 0]
 
 
-def rebuilt_kernel(pre, back, out):
+def split_kernel(back, grad, held_out, grad_out, late_out):
+    held_out[...] = back[0, 1]
+    grad_out[...] = grad[0, 0]
+    late_out[0] = back[0, 0]
+    late_out[1] = grad[0, 1]
+
+
+def rebuilt_kernel(pre, lower, late, wrap, out):
     t = pre[...]
-    out[0, 0] = back[0, 1]
-    out[0, 1] = (back[0, 0].astype(F32) - t * jax.nn.sigmoid(t)).astype(BF16)
-
-
-def grad_kernel(exchange, other, out):
+    out[0, 0] = lower[...]
+    out[0, 1] = ((late[0] + wrap[0]).astype(F32) - t * jax.nn.sigmoid(t)).astype(BF16)
+
+
+def grad_kernel(own, dp_1, dp_2, dp_3, swapped, out):
     _, _, core = places()
     half = out.shape[1] // 2
-    hidden = exchange[:, 1].reshape(-1, exchange.shape[-1])
-    even, odd = by_parity(core, exchange[:, 0], other[...])
-    out[0, :half] = tn(even.reshape(-1, half), hidden).astype(BF16)
-    out[0, half:] = tn(odd.reshape(-1, half), hidden).astype(BF16)
+    hidden = jnp.concatenate([own[2], dp_1[1], dp_2[1], dp_3[1]])
+    mine = jnp.concatenate([own[0], dp_1[0], dp_2[0], dp_3[0]])
+    other = jnp.concatenate([own[1], swapped[0], swapped[1], swapped[2]])
+    even, odd = by_parity(core, mine, other)
+    out[0, :half] = tn(even, hidden).astype(BF16)
+    out[0, half:] = tn(odd, hidden).astype(BF16)
+
+
+def share_kernel(dp_1, dp_2, dp_3, out):
+    out[0] = dp_1[0]
+    out[1] = dp_2[0]
+    out[2] = dp_3[0]
+
+
+def stack_kernel(first, second, out):
+    out[0] = first[...]
+    out[1] = second[...]
 
 
 def near_kernel(keep, received, out):
@@ -126,11 +149,11 @@
     out[...] = (keep[0, 1].astype(F32) + received[0, 1].astype(F32) + near[1].astype(F32)).astype(BF16)
 
 
-def last_kernel(length, keep, received, near, far, grad, out):
+def last_kernel(length, keep, received, near, far, upper, late, wrap, out):
     live = lax.broadcasted_iota(jnp.int32, far.shape, 0) < length[0, 0]
     through = keep[0, 0].astype(F32) + received[0, 0].astype(F32) + near[0].astype(F32) + far[...].astype(F32)
-    out[0, 0] = (jnp.where(live, grad[0, 1].astype(F32), 0.0) + through).astype(BF16)
-    out[0, 1] = jnp.where(live, grad[0, 0].astype(F32), 0.0).astype(BF16)
+    out[0, 0] = (jnp.where(live, (late[1] + wrap[1]).astype(F32), 0.0) + through).astype(BF16)
+    out[0, 1] = jnp.where(live, upper[...].astype(F32), 0.0).astype(BF16)
 
 
 def run(kernel, outs, args, flops=0, scalars=0, mib=8):
@@ -140,7 +163,7 @@
     return pl.pallas_call(
         kernel,
         out_shape=outs,
-        in_specs=[smem] * scalars + [vmem] * (len(args) - scalars),
+        in_specs=[smem if n < scalars else vmem for n in range(len(args))],
         out_specs=jax.tree.map(lambda _: vmem, outs),
         cost_estimate=pl.CostEstimate(flops=flops, transcendentals=0, bytes_accessed=moved),
         compiler_params=pltpu.CompilerParams(vmem_limit_bytes=mib * 2**20),
@@ -149,7 +172,7 @@
 
 def gathered(block):
     far = exchanged(block, 4)
-    own_pair = jnp.stack([block, far])
+    own_pair = run(stack_kernel, jax.ShapeDtypeStruct((2, *block.shape), BF16), (block, far))
     near_pair = exchanged(own_pair, 2)
     other_own = exchanged(own_pair, 1)
     other_near = exchanged(near_pair, 1)
@@ -163,39 +186,52 @@
     half = depth // 2
     shape = jax.ShapeDtypeStruct
     pair = shape((1, 2, tokens, width), BF16)
+    block = shape((tokens, width), BF16)
+    two = shape((2, tokens, width), BF16)
+    three = shape((3, tokens, width), BF16)
     product = 2 * tokens * width * 4 * depth
 
     prev = shifted(own, "dp", 1)
     nxt = shifted(own, "dp", -1)
-    back = shifted(sent_back, "section", -1)
+    held_out, grad_out, late_out = run(split_kernel, (block, block, two), (sent_back, sent_grad))
+    back_lower = shifted(held_out, "section", -1)
     inbound = shifted(sent_out, "section", 1)
-    grad = shifted(sent_grad, "section", -1)
+    grad_upper = shifted(grad_out, "section", -1)
+    count = lax.axis_size("section")
+    rank = count // 2
+    across = lax.ppermute(late_out, "section", [(0, rank + 1), (rank, 1)])
+    late = lax.ppermute(late_out, "section", [(i, i - 1) for i in range(count) if i % rank])
+    late_wrap = lax.ppermute(across, "section", [(rank + 1, count - 1), (1, rank - 1)])
     far_lo = shifted(prev[:half], "dp", 1)
     far_hi = shifted(nxt[half:], "dp", -1)
     weights = (own, prev, nxt, far_lo, far_hi)
-    held = gathered(back[0, 1])
-    new = gathered(inbound[0, 0])
+    upper_in = inbound[0, 0]
+    held = gathered(back_lower)
+    new = gathered(upper_in)
 
     terms = shape((2, 2, tokens, width), BF16)
-    pre_held, keep, send, share = run(
+    keep, send, own_share, *to_dp, pre_held = run(
         held_kernel,
-        (shape((tokens, width), F32), terms, terms, shape((4, 2, tokens, width), BF16)),
-        (lengths, *held, *weights, grad),
+        (terms, terms, three, two, two, two, shape((tokens, width), F32)),
+        (lengths, *held, *weights, grad_upper),
         flops=2 * product,
         scalars=1,
         mib=20,
     )
     received = exchanged(send, 1)
-    exchange = lax.all_to_all(share, "dp", 0, 0, tiled=True)
+    from_dp = []
+    for distance in (1, 2, 3):
+        from_dp.append(shifted(to_dp[distance - 1], "dp", distance))
     near_sum = run(near_kernel, shape((2, tokens, width), BF16), (keep, received))
     near = exchanged(near_sum, 2)
     emitted = run(new_kernel, pair, (*new, *weights, inbound), flops=product, mib=16)
     far_sum = run(far_kernel, shape((tokens, width), BF16), (keep, received, near))
     far = exchanged(far_sum, 4)
-    rebuilt = run(rebuilt_kernel, pair, (pre_held, back), flops=tokens * width)
-    other = exchanged(exchange[:, 0], 1)
-    weight_grad = run(grad_kernel, shape(weight.shape, BF16), (exchange, other), flops=product, mib=16)
-    input_grad = run(last_kernel, pair, (lengths, keep, received, near, far, grad), scalars=1)
+    rebuilt = run(rebuilt_kernel, pair, (pre_held, back_lower, late, late_wrap), flops=tokens * width)
+    shares = run(share_kernel, three, from_dp)
+    other = exchanged(shares, 1)
+    weight_grad = run(grad_kernel, shape(weight.shape, BF16), (own_share, *from_dp, other), flops=product, mib=16)
+    input_grad = run(last_kernel, pair, (lengths, keep, received, near, far, grad_upper, late, late_wrap), scalars=1)
     return emitted, rebuilt, input_grad, weight_grad
 
 

time: 161 us -> 154 us (0.957)
  waiting for transfers between devices: 64.9 us -> 56 us
  starting transfers between devices: 79.3 us -> 85.5 us
  local copies, waits for them, and re-layouts: 3.8 us -> 2.08 us
    ppermute x7 -> x10, starting transfers between devices: 40.9 us -> 52.1 us  [shifted(): return lax.ppermute(block, axis, route)]
    ppermute x12, waiting for transfers between devices: 25.9 us -> 19.1 us  [exchanged(): lax.ppermute(block, 'tensor', [(i, i ^ flip) for i in range(lax.axis_size...]
    ppermute x7 -> x10, waiting for transfers between devices: 39 us -> 33.5 us  [shifted(): return lax.ppermute(block, axis, route)]
    all_to_all x1 -> x0, starting transfers between devices: 5.15 us -> none  [local(): exchange = lax.all_to_all(share, 'dp', 0, 0, tiled=True)]
    ppermute x0 -> x3, waiting for transfers between devices: none -> 3.42 us  [the longest x1 2.98 us: local(): lax.ppermute(late_out, 'section', [(i, i - 1) for i in range(count) if i...]
    ppermute x0 -> x3, starting transfers between devices: none -> 3.27 us  [the longest x1 1.3 us: local(): across = lax.ppermute(late_out, 'section', [(0, rank + 1), (rank, 1)])]
    ppermute x12, starting transfers between devices: 33.3 us -> 30.1 us  [exchanged(): lax.ppermute(block, 'tensor', [(i, i ^ flip) for i in range(lax.axis_size...]
    unnamed x38 -> x8, local copies, waits for them, and re-layouts: 3.62 us -> 2 us
  transfers between devices with their start and end apart: 20 -> 25, of which waited for: 7 -> 11; matrix products, arithmetic and copies ran while one was open for 1% -> 0% of each run, Pallas kernels for 3% -> 5%
where the time goes in v2:
time: 154 us
  starting transfers between devices  85.5 us (56%)
  waiting for transfers between devices  56 us (36%)
  Pallas kernels  8.38 us (5%)
  local copies, waits for them, and re-layouts  2.08 us (1%)
  between operations  1.67 us (1%)
    ppermute x10, starting transfers between devices, shifted(): return lax.ppermute(block, axis, route)  52.1 us
    ppermute x10, waiting for transfers between devices, shifted(): return lax.ppermute(block, axis, route)  33.5 us
    ppermute x12, starting transfers between devices, exchanged(): lax.ppermute(block, 'tensor', [(i, i ^ flip) for i in range(lax.axis_size...  30.1 us
    ppermute x12, waiting for transfers between devices, exchanged(): lax.ppermute(block, 'tensor', [(i, i ^ flip) for i in range(lax.axis_size...  19.1 us
    pallas_call x11, Pallas kernels, run(): pl.pallas_call(kernel, out_shape=outs, in_specs=[smem if n < scalars else...  8.38 us
  transfers between devices with their start and end apart: 25, of which 11 were waited for; matrix products, arithmetic and copies ran while one was open for 0% of the time, Pallas kernels for 5%

profile of v2, /device:TPU:6, one launch (start us, length us, event | category | flops | bytes accessed | tf_op | source)
XLA Modules:
  0.0 153.6 jit_solution(10988257480744247960)
XLA Ops:
  0.6 7.7 %collective-permute-start.5 = (bf16[1024,512]{1,0:T(8,128)(2,1)}, bf16[1024,512]{1,0:T(8,128)(2,1)S(1)}, u32[]{:S(2)}, u32[]{:S(2)}) collective-permute-start(bf16[1024,512]{1,0:T(8,128)(2,1)} %bitcast.3), channel_id=1, source_target_pairs={{24,0},{0,8},{8,16},{16,24},{25,1},{1,9},{9,17},{17,25},{26,2},{2,... | collective-permute-start | bytes 3145736 | tf_op jit(solution)/shard_map/ppermute | solution.py:16
  8.4 1.9 %collective-permute-start.6 = (bf16[1024,512]{1,0:T(8,128)(2,1)}, bf16[1024,512]{1,0:T(8,128)(2,1)S(1)}, u32[]{:S(2)}, u32[]{:S(2)}) collective-permute-start(bf16[1024,512]{1,0:T(8,128)(2,1)} %bitcast.4), channel_id=1, source_target_pairs={{8,0},{16,8},{24,16},{0,24},{9,1},{17,9},{25,17},{1,25},{10,2},{18... | collective-permute-start | bytes 3145736 | tf_op jit(solution)/shard_map/ppermute | solution.py:16
  10.3 1.0 copy-done.1
  11.3 1.0 copy-done.2
  12.3 0.1 shard_map.86
  12.4 10.0 %collective-permute-start.9 = (bf16[192,512]{1,0:T(8,128)(2,1)S(1)}, bf16[192,512]{1,0:T(8,128)(2,1)S(1)}, u32[]{:S(2)}, u32[]{:S(2)}) collective-permute-start(bf16[192,512]{1,0:T(8,128)(2,1)S(1)} %get-tuple-element.14), channel_id=1, source_target_pairs={{32,0},{64,32},{96,64},{128,96},{160,128},{192,160},{224,192},{256... | collective-permute-start | bytes 589832 | tf_op jit(solution)/shard_map/ppermute | solution.py:16
  22.4 5.2 %collective-permute-done.9.first.lower = bf16[192,512]{1,0:T(8,128)(2,1)S(1)} collective-permute-done((bf16[192,512]{1,0:T(8,128)(2,1)S(1)}, bf16[192,512]{1,0:T(8,128)(2,1)S(1)}, u32[]{:S(2)}, u32[]{:S(2)}) %collective-permute-start.9) | collective-permute-done | bytes 196640 | tf_op jit(solution)/shard_map/ppermute | solution.py:16
  27.6 4.0 %collective-permute-start.10 = (bf16[192,512]{1,0:T(8,128)(2,1)S(1)}, bf16[192,512]{1,0:T(8,128)(2,1)S(1)}, u32[]{:S(2)}, u32[]{:S(2)}) collective-permute-start(bf16[192,512]{1,0:T(8,128)(2,1)S(1)} %collective-permute-done.9.first.lower), channel_id=1, source_target_pairs={{0,4},{1,5},{2,6},{3,7},{4,0},{5,1},{6,2},{7,3},{8,12},{9,13},{10,... | collective-permute-start | bytes 589832 | tf_op jit(solution)/shard_map/ppermute | solution.py:20
  31.6 7.0 %collective-permute-done.10.second = bf16[192,512]{1,0:T(8,128)(2,1)S(1)} collective-permute-done((bf16[192,512]{1,0:T(8,128)(2,1)S(1)}, bf16[192,512]{1,0:T(8,128)(2,1)S(1)}, u32[]{:S(2)}, u32[]{:S(2)}) %collective-permute-start.10) | collective-permute-done | bytes 196640 | tf_op jit(solution)/shard_map/ppermute | solution.py:20
  38.6 0.0 copy-start
  38.6 2.2 %collective-permute-start.11 = (bf16[2,192,512]{2,1,0:T(8,128)(2,1)S(1)}, bf16[2,192,512]{2,1,0:T(8,128)(2,1)S(1)}, u32[]{:S(2)}, u32[]{:S(2)}) collective-permute-start(bf16[2,192,512]{2,1,0:T(8,128)(2,1)S(1)} %shard_map.87.mine_a), channel_id=1, source_target_pairs={{0,2},{1,3},{2,0},{3,1},{4,6},{5,7},{6,4},{7,5},{8,10},{9,11},{10,... | collective-permute-start | bytes 1179656 | tf_op jit(solution)/shard_map/ppermute | solution.py:20
  40.9 0.0 copy-start.3
  40.9 3.7 %collective-permute-start.7 = (bf16[512,512]{1,0:T(8,128)(2,1)S(1)}, bf16[512,512]{1,0:T(8,128)(2,1)S(1)}, u32[]{:S(2)}, u32[]{:S(2)}) collective-permute-start(bf16[512,512]{1,0:T(8,128)(2,1)S(1)} %slice.13), channel_id=1, source_target_pairs={{24,0},{0,8},{8,16},{16,24},{25,1},{1,9},{9,17},{17,25},{26,2},{2,... | collective-permute-start | bytes 1572872 | tf_op jit(solution)/shard_map/ppermute | solution.py:16
  44.7 2.2 %collective-permute-start.8 = (bf16[512,512]{1,0:T(8,128)(2,1)S(1)}, bf16[512,512]{1,0:T(8,128)(2,1)S(1)}, u32[]{:S(2)}, u32[]{:S(2)}) collective-permute-start(bf16[512,512]{1,0:T(8,128)(2,1)S(1)} %slice.14), channel_id=1, source_target_pairs={{8,0},{16,8},{24,16},{0,24},{9,1},{17,9},{25,17},{1,25},{10,2},{18... | collective-permute-start | bytes 1572872 | tf_op jit(solution)/shard_map/ppermute | solution.py:16
  46.9 1.9 %collective-permute-start.12 = (bf16[2,192,512]{2,1,0:T(8,128)(2,1)S(1)}, bf16[2,192,512]{2,1,0:T(8,128)(2,1)S(1)}, u32[]{:S(2)}, u32[]{:S(2)}) collective-permute-start(bf16[2,192,512]{2,1,0:T(8,128)(2,1)S(1)} %shard_map.87.mine_a), channel_id=1, source_target_pairs={{0,1},{1,0},{2,3},{3,2},{4,5},{5,4},{6,7},{7,6},{8,9},{9,8},{10,11... | collective-permute-start | bytes 1179656 | tf_op jit(solution)/shard_map/ppermute | solution.py:20
  48.9 1.9 %collective-permute-done.11.mine_b = bf16[2,192,512]{2,1,0:T(8,128)(2,1)S(1)} collective-permute-done((bf16[2,192,512]{2,1,0:T(8,128)(2,1)S(1)}, bf16[2,192,512]{2,1,0:T(8,128)(2,1)S(1)}, u32[]{:S(2)}, u32[]{:S(2)}) %collective-permute-start.11) | collective-permute-done | bytes 393248 | tf_op jit(solution)/shard_map/ppermute | solution.py:20
  50.7 1.9 %collective-permute-start.13 = (bf16[2,192,512]{2,1,0:T(8,128)(2,1)S(1)}, bf16[2,192,512]{2,1,0:T(8,128)(2,1)S(1)}, u32[]{:S(2)}, u32[]{:S(2)}) collective-permute-start(bf16[2,192,512]{2,1,0:T(8,128)(2,1)S(1)} %collective-permute-done.11.mine_b), channel_id=1, source_target_pairs={{0,1},{1,0},{2,3},{3,2},{4,5},{5,4},{6,7},{7,6},{8,9},{9,8},{10,11... | collective-permute-start | bytes 1179656 | tf_op jit(solution)/shard_map/ppermute | solution.py:20
  52.6 13.3 %collective-permute-start.14 = (bf16[192,512]{1,0:T(8,128)(2,1)S(1)}, bf16[192,512]{1,0:T(8,128)(2,1)S(1)}, u32[]{:S(2)}, u32[]{:S(2)}) collective-permute-start(bf16[192,512]{1,0:T(8,128)(2,1)S(1)} %get-tuple-element.15), channel_id=1, source_target_pairs={{32,0},{64,32},{96,64},{128,96},{160,128},{192,160},{224,192},{256... | collective-permute-start | bytes 589832 | tf_op jit(solution)/shard_map/ppermute | solution.py:16
  66.6 5.8 %collective-permute-done.14.grad.upper = bf16[192,512]{1,0:T(8,128)(2,1)S(1)} collective-permute-done((bf16[192,512]{1,0:T(8,128)(2,1)S(1)}, bf16[192,512]{1,0:T(8,128)(2,1)S(1)}, u32[]{:S(2)}, u32[]{:S(2)}) %collective-permute-start.14) | collective-permute-done | bytes 196640 | tf_op jit(solution)/shard_map/ppermute | solution.py:16
  72.4 1.9 %collective-permute-start = (bf16[1,2,192,512]{3,2,1,0:T(8,128)(2,1)S(1)}, bf16[1,2,192,512]{3,2,1,0:T(8,128)(2,1)S(1)}, u32[]{:S(2)}, u32[]{:S(2)}) collective-permute-start(bf16[1,2,192,512]{3,2,1,0:T(8,128)(2,1)S(1)} %copy-done.3), channel_id=1, source_target_pairs={{480,0},{0,32},{32,64},{64,96},{96,128},{128,160},{160,192},{192,2... | collective-permute-start | bytes 1179656 | tf_op jit(solution)/shard_map/ppermute | solution.py:16
  74.3 2.5 %shard_map.88 = (bf16[2,2,192,512]{3,2,1,0:T(8,128)(2,1)S(1)}, bf16[2,2,192,512]{3,2,1,0:T(8,128)(2,1)S(1)}, bf16[3,192,512]{2,1,0:T(8,128)(2,1)S(1)}, bf16[2,19...) custom-call(s32[1,1]{1,0:T(1,128)S(6)} %copy.9.length, ...), custom_call_target="tpu_custom_call" | custom-call | flops 1610612736 | bytes 5963780 | tf_op jit(solution)/shard_map/pallas_call | solution.py:163
  76.9 1.9 %collective-permute-start.18 = (bf16[2,2,192,512]{3,2,1,0:T(8,128)(2,1)S(1)}, bf16[2,2,192,512]{3,2,1,0:T(8,128)(2,1)S(1)}, u32[]{:S(2)}, u32[]{:S(2)}) collective-permute-start(bf16[2,2,192,512]{3,2,1,0:T(8,128)(2,1)S(1)} %get-tuple-element.19), channel_id=1, source_target_pairs={{0,1},{1,0},{2,3},{3,2},{4,5},{5,4},{6,7},{7,6},{8,9},{9,8},{10,11... | collective-permute-start | bytes 2359304 | tf_op jit(solution)/shard_map/ppermute | solution.py:20
  78.8 3.6 %collective-permute-start.21 = (bf16[2,192,512]{2,1,0:T(8,128)(2,1)S(1)}, bf16[2,192,512]{2,1,0:T(8,128)(2,1)S(1)}, u32[]{:S(2)}, u32[]{:S(2)}) collective-permute-start(bf16[2,192,512]{2,1,0:T(8,128)(2,1)S(1)} %get-tuple-element.21), channel_id=1, source_target_pairs={{24,0},{0,8},{8,16},{16,24},{25,1},{1,9},{9,17},{17,25},{26,2},{2,... | collective-permute-start | bytes 1179656 | tf_op jit(solution)/shard_map/ppermute | solution.py:16
  82.4 18.2 %collective-permute-done.inbound = bf16[1,2,192,512]{3,2,1,0:T(8,128)(2,1)S(1)} collective-permute-done((bf16[1,2,192,512]{3,2,1,0:T(8,128)(2,1)S(1)}, bf16[1,2,192,512]{3,2,1,0:T(8,128)(2,1)S(1)}, u32[]{:S(2)}, u32[]{:S(2)}) %collective-permute-start) | collective-permute-done | bytes 393248 | tf_op jit(solution)/shard_map/ppermute | solution.py:16
  100.6 1.9 %collective-permute-start.1 = (bf16[192,512]{1,0:T(8,128)(2,1)S(1)}, bf16[192,512]{1,0:T(8,128)(2,1)S(1)}, u32[]{:S(2)}, u32[]{:S(2)}) collective-permute-start(bf16[192,512]{1,0:T(8,128)(2,1)S(1)} %slice_bitcast_fusion.first), channel_id=1, source_target_pairs={{0,4},{1,5},{2,6},{3,7},{4,0},{5,1},{6,2},{7,3},{8,12},{9,13},{10,... | collective-permute-start | bytes 589832 | tf_op jit(solution)/shard_map/ppermute | solution.py:20
  102.5 3.3 %collective-permute-start.22 = (bf16[2,192,512]{2,1,0:T(8,128)(2,1)S(1)}, bf16[2,192,512]{2,1,0:T(8,128)(2,1)S(1)}, u32[]{:S(2)}, u32[]{:S(2)}) collective-permute-start(bf16[2,192,512]{2,1,0:T(8,128)(2,1)S(1)} %get-tuple-element.22), channel_id=1, source_target_pairs={{16,0},{24,8},{0,16},{8,24},{17,1},{25,9},{1,17},{9,25},{18,2},{26... | collective-permute-start | bytes 1179656 | tf_op jit(solution)/shard_map/ppermute | solution.py:16
  105.8 4.4 %collective-permute-start.23 = (bf16[2,192,512]{2,1,0:T(8,128)(2,1)S(1)}, bf16[2,192,512]{2,1,0:T(8,128)(2,1)S(1)}, u32[]{:S(2)}, u32[]{:S(2)}) collective-permute-start(bf16[2,192,512]{2,1,0:T(8,128)(2,1)S(1)} %get-tuple-element.23), channel_id=1, source_target_pairs={{8,0},{16,8},{24,16},{0,24},{9,1},{17,9},{25,17},{1,25},{10,2},{18... | collective-permute-start | bytes 1179656 | tf_op jit(solution)/shard_map/ppermute | solution.py:16
  110.2 1.9 %collective-permute-done.1.second = bf16[192,512]{1,0:T(8,128)(2,1)S(1)} collective-permute-done((bf16[192,512]{1,0:T(8,128)(2,1)S(1)}, bf16[192,512]{1,0:T(8,128)(2,1)S(1)}, u32[]{:S(2)}, u32[]{:S(2)}) %collective-permute-start.1) | collective-permute-done | bytes 196640 | tf_op jit(solution)/shard_map/ppermute | solution.py:20
  112.1 1.3 collective-permute-start.16
  113.5 1.9 %collective-permute-start.2 = (bf16[2,192,512]{2,1,0:T(8,128)(2,1)S(1)}, bf16[2,192,512]{2,1,0:T(8,128)(2,1)S(1)}, u32[]{:S(2)}, u32[]{:S(2)}) collective-permute-start(bf16[2,192,512]{2,1,0:T(8,128)(2,1)S(1)} %shard_map.84.mine_a), channel_id=1, source_target_pairs={{0,2},{1,3},{2,0},{3,1},{4,6},{5,7},{6,4},{7,5},{8,10},{9,11},{10,... | collective-permute-start | bytes 1179656 | tf_op jit(solution)/shard_map/ppermute | solution.py:20
  115.4 0.1 shard_map.90
  115.5 3.9 %collective-permute-start.19 = (bf16[2,192,512]{2,1,0:T(8,128)(2,1)S(1)}, bf16[2,192,512]{2,1,0:T(8,128)(2,1)S(1)}, u32[]{:S(2)}, u32[]{:S(2)}) collective-permute-start(bf16[2,192,512]{2,1,0:T(8,128)(2,1)S(1)} %shard_map.90), channel_id=1, source_target_pairs={{0,2},{1,3},{2,0},{3,1},{4,6},{5,7},{6,4},{7,5},{8,10},{9,11},{10,... | collective-permute-start | bytes 1179656 | tf_op jit(solution)/shard_map/ppermute | solution.py:20
  119.4 4.4 %collective-permute-done.23.dp_3 = bf16[2,192,512]{2,1,0:T(8,128)(2,1)S(1)} collective-permute-done((bf16[2,192,512]{2,1,0:T(8,128)(2,1)S(1)}, bf16[2,192,512]{2,1,0:T(8,128)(2,1)S(1)}, u32[]{:S(2)}, u32[]{:S(2)}) %collective-permute-start.23) | collective-permute-done | bytes 393248 | tf_op jit(solution)/shard_map/ppermute | solution.py:16
  123.9 1.9 %collective-permute-start.24 = (bf16[3,192,512]{2,1,0:T(8,128)(2,1)S(1)}, bf16[3,192,512]{2,1,0:T(8,128)(2,1)S(1)}, u32[]{:S(2)}, u32[]{:S(2)}) collective-permute-start(bf16[3,192,512]{2,1,0:T(8,128)(2,1)S(1)} %shard_map.93), channel_id=1, source_target_pairs={{0,1},{1,0},{2,3},{3,2},{4,5},{5,4},{6,7},{7,6},{8,9},{9,8},{10,11... | collective-permute-start | bytes 1769480 | tf_op jit(solution)/shard_map/ppermute | solution.py:20
  125.8 1.3 collective-permute-start.15
  127.1 0.4 collective-permute-done.16
  127.5 0.7 collective-permute-start.17
  128.2 2.0 %collective-permute-start.3 = (bf16[2,192,512]{2,1,0:T(8,128)(2,1)S(1)}, bf16[2,192,512]{2,1,0:T(8,128)(2,1)S(1)}, u32[]{:S(2)}, u32[]{:S(2)}) collective-permute-start(bf16[2,192,512]{2,1,0:T(8,128)(2,1)S(1)} %shard_map.84.mine_a), channel_id=1, source_target_pairs={{0,1},{1,0},{2,3},{3,2},{4,5},{5,4},{6,7},{7,6},{8,9},{9,8},{10,11... | collective-permute-start | bytes 1179656 | tf_op jit(solution)/shard_map/ppermute | solution.py:20
  130.2 4.5 %collective-permute-done.19.near = bf16[2,192,512]{2,1,0:T(8,128)(2,1)S(1)} collective-permute-done((bf16[2,192,512]{2,1,0:T(8,128)(2,1)S(1)}, bf16[2,192,512]{2,1,0:T(8,128)(2,1)S(1)}, u32[]{:S(2)}, u32[]{:S(2)}) %collective-permute-start.19) | collective-permute-done | bytes 393248 | tf_op jit(solution)/shard_map/ppermute | solution.py:20
  134.7 1.9 %collective-permute-start.4 = (bf16[2,192,512]{2,1,0:T(8,128)(2,1)S(1)}, bf16[2,192,512]{2,1,0:T(8,128)(2,1)S(1)}, u32[]{:S(2)}, u32[]{:S(2)}) collective-permute-start(bf16[2,192,512]{2,1,0:T(8,128)(2,1)S(1)} %collective-permute-done.2.mine_b), channel_id=1, source_target_pairs={{0,1},{1,0},{2,3},{3,2},{4,5},{5,4},{6,7},{7,6},{8,9},{9,8},{10,11... | collective-permute-start | bytes 1179656 | tf_op jit(solution)/shard_map/ppermute | solution.py:20
  136.6 0.1 shard_map.91
  136.7 3.0 %collective-permute-done.15.late = bf16[2,192,512]{2,1,0:T(8,128)(2,1)S(1)} collective-permute-done((bf16[2,192,512]{2,1,0:T(8,128)(2,1)S(1)}, bf16[2,192,512]{2,1,0:T(8,128)(2,1)S(1)}, u32[]{:S(2)}, u32[]{:S(2)}) %collective-permute-start.15) | collective-permute-done | bytes 393248 | tf_op jit(solution)/shard_map/ppermute | solution.py:203
  139.7 4.5 %collective-permute-start.20 = (bf16[192,512]{1,0:T(8,128)(2,1)S(1)}, bf16[192,512]{1,0:T(8,128)(2,1)S(1)}, u32[]{:S(2)}, u32[]{:S(2)}) collective-permute-start(bf16[192,512]{1,0:T(8,128)(2,1)S(1)} %shard_map.91), channel_id=1, source_target_pairs={{0,4},{1,5},{2,6},{3,7},{4,0},{5,1},{6,2},{7,3},{8,12},{9,13},{10,... | collective-permute-start | bytes 589832 | tf_op jit(solution)/shard_map/ppermute | solution.py:20
  144.2 0.8 shard_map.89
  145.1 1.8 %shard_map.85 = bf16[1,2,192,512]{3,2,1,0:T(8,128)(2,1)} custom-call(bf16[2,192,512]{2,1,0:T(8,128)(2,1)S(1)} %shard_map.84.mine_a, bf16[2,192,512]{2,1,0:T(8,128)(2,1)S(1)} %collective-permute-done.2.mine_b, bf16[2,192,512]{2,1,0:T(8,128)(2,1)S(1)} %collective-permute-done.3.other_a, bf16[2,192,512]{2,1,0:T(8,128)(2,1)S(1)} %collective-permute-done.4.other_b, ...), custom_call_target="tpu_custom_call" | custom-call | flops 805306368 | bytes 6160384 | tf_op jit(solution)/shard_map/pallas_call | solution.py:163
  146.9 2.0 %shard_map.94 = bf16[1,1024,512]{2,1,0:T(8,128)(2,1)} custom-call(bf16[3,192,512]{2,1,0:T(8,128)(2,1)S(1)} %get-tuple-element.20.own, bf16[2,192,512]{2,1,0:T(8,128)(2,1)S(1)} %collective-permute-done.21.dp_1, bf16[2,192,512]{2,1,0:T(8,128)(2,1)S(1)} %collective-permute-done.22.dp_2, bf16[2,192,512]{2,1,0:T(8,128)(2,1)S(1)} %collective-permute-done.23.dp_3, ...), custom_call_target="tpu_custom_call" | custom-call | flops 805306368 | bytes 2359296 | tf_op jit(solution)/shard_map/pallas_call | solution.py:163
  148.8 3.8 %collective-permute-done.20.far = bf16[192,512]{1,0:T(8,128)(2,1)S(1)} collective-permute-done((bf16[192,512]{1,0:T(8,128)(2,1)S(1)}, bf16[192,512]{1,0:T(8,128)(2,1)S(1)}, u32[]{:S(2)}, u32[]{:S(2)}) %collective-permute-start.20) | collective-permute-done | bytes 196640 | tf_op jit(solution)/shard_map/ppermute | solution.py:20
  152.6 0.9 shard_map.92
  (24 shorter events, 0.2 us)
Async XLA Ops:
  0.6 40.2 %collective-permute-start.5 = (bf16[1024,512]{1,0:T(8,128)(2,1)}, bf16[1024,512]{1,0:T(8,128)(2,1)S(1)}, u32[]{:S(2)}, u32[]{:S(2)}) collective-permute-start(bf16[1024,512]{1,0:T(8,128)(2,1)} %bitcast.3), channel_id=1, source_target_pairs={{24,0},{0,8},{8,16},{16,24},{25,1},{1,9},{9,17},{17,25},{26,2},{2,... | collective-permute-start | bytes 3145736 | tf_op jit(solution)/shard_map/ppermute | solution.py:16
  8.4 36.3 %collective-permute-start.6 = (bf16[1024,512]{1,0:T(8,128)(2,1)}, bf16[1024,512]{1,0:T(8,128)(2,1)S(1)}, u32[]{:S(2)}, u32[]{:S(2)}) collective-permute-start(bf16[1024,512]{1,0:T(8,128)(2,1)} %bitcast.4), channel_id=1, source_target_pairs={{8,0},{16,8},{24,16},{0,24},{9,1},{17,9},{25,17},{1,25},{10,2},{18... | collective-permute-start | bytes 3145736 | tf_op jit(solution)/shard_map/ppermute | solution.py:16
  10.3 1.0 copy-start.1
  11.3 1.0 copy-start.2
  12.4 15.2 %collective-permute-start.9 = (bf16[192,512]{1,0:T(8,128)(2,1)S(1)}, bf16[192,512]{1,0:T(8,128)(2,1)S(1)}, u32[]{:S(2)}, u32[]{:S(2)}) collective-permute-start(bf16[192,512]{1,0:T(8,128)(2,1)S(1)} %get-tuple-element.14), channel_id=1, source_target_pairs={{32,0},{64,32},{96,64},{128,96},{160,128},{192,160},{224,192},{256... | collective-permute-start | bytes 589832 | tf_op jit(solution)/shard_map/ppermute | solution.py:16
  27.6 11.0 %collective-permute-start.10 = (bf16[192,512]{1,0:T(8,128)(2,1)S(1)}, bf16[192,512]{1,0:T(8,128)(2,1)S(1)}, u32[]{:S(2)}, u32[]{:S(2)}) collective-permute-start(bf16[192,512]{1,0:T(8,128)(2,1)S(1)} %collective-permute-done.9.first.lower), channel_id=1, source_target_pairs={{0,4},{1,5},{2,6},{3,7},{4,0},{5,1},{6,2},{7,3},{8,12},{9,13},{10,... | collective-permute-start | bytes 589832 | tf_op jit(solution)/shard_map/ppermute | solution.py:20
  38.6 35.7 %copy-start = (bf16[1,1024,512]{2,1,0:T(8,128)(2,1)S(1)}, bf16[1,1024,512]{2,1,0:T(8,128)(2,1)}, u32[]{:S(2)}) copy-start(bf16[1,1024,512]{2,1,0:T(8,128)(2,1)} %param.9) | copy-start | bytes 3145732
  38.6 12.1 %collective-permute-start.11 = (bf16[2,192,512]{2,1,0:T(8,128)(2,1)S(1)}, bf16[2,192,512]{2,1,0:T(8,128)(2,1)S(1)}, u32[]{:S(2)}, u32[]{:S(2)}) collective-permute-start(bf16[2,192,512]{2,1,0:T(8,128)(2,1)S(1)} %shard_map.87.mine_a), channel_id=1, source_target_pairs={{0,2},{1,3},{2,0},{3,1},{4,6},{5,7},{6,4},{7,5},{8,10},{9,11},{10,... | collective-permute-start | bytes 1179656 | tf_op jit(solution)/shard_map/ppermute | solution.py:20
  40.9 31.5 %copy-start.3 = (bf16[1,2,192,512]{3,2,1,0:T(8,128)(2,1)S(1)}, bf16[1,2,192,512]{3,2,1,0:T(8,128)(2,1)}, u32[]{:S(2)}) copy-start(bf16[1,2,192,512]{3,2,1,0:T(8,128)(2,1)} %param.5) | copy-start | bytes 1179652
  40.9 33.4 %collective-permute-start.7 = (bf16[512,512]{1,0:T(8,128)(2,1)S(1)}, bf16[512,512]{1,0:T(8,128)(2,1)S(1)}, u32[]{:S(2)}, u32[]{:S(2)}) collective-permute-start(bf16[512,512]{1,0:T(8,128)(2,1)S(1)} %slice.13), channel_id=1, source_target_pairs={{24,0},{0,8},{8,16},{16,24},{25,1},{1,9},{9,17},{17,25},{26,2},{2,... | collective-permute-start | bytes 1572872 | tf_op jit(solution)/shard_map/ppermute | solution.py:16
  44.7 29.6 %collective-permute-start.8 = (bf16[512,512]{1,0:T(8,128)(2,1)S(1)}, bf16[512,512]{1,0:T(8,128)(2,1)S(1)}, u32[]{:S(2)}, u32[]{:S(2)}) collective-permute-start(bf16[512,512]{1,0:T(8,128)(2,1)S(1)} %slice.14), channel_id=1, source_target_pairs={{8,0},{16,8},{24,16},{0,24},{9,1},{17,9},{25,17},{1,25},{10,2},{18... | collective-permute-start | bytes 1572872 | tf_op jit(solution)/shard_map/ppermute | solution.py:16
  46.9 27.3 %collective-permute-start.12 = (bf16[2,192,512]{2,1,0:T(8,128)(2,1)S(1)}, bf16[2,192,512]{2,1,0:T(8,128)(2,1)S(1)}, u32[]{:S(2)}, u32[]{:S(2)}) collective-permute-start(bf16[2,192,512]{2,1,0:T(8,128)(2,1)S(1)} %shard_map.87.mine_a), channel_id=1, source_target_pairs={{0,1},{1,0},{2,3},{3,2},{4,5},{5,4},{6,7},{7,6},{8,9},{9,8},{10,11... | collective-permute-start | bytes 1179656 | tf_op jit(solution)/shard_map/ppermute | solution.py:20
  50.7 23.6 %collective-permute-start.13 = (bf16[2,192,512]{2,1,0:T(8,128)(2,1)S(1)}, bf16[2,192,512]{2,1,0:T(8,128)(2,1)S(1)}, u32[]{:S(2)}, u32[]{:S(2)}) collective-permute-start(bf16[2,192,512]{2,1,0:T(8,128)(2,1)S(1)} %collective-permute-done.11.mine_b), channel_id=1, source_target_pairs={{0,1},{1,0},{2,3},{3,2},{4,5},{5,4},{6,7},{7,6},{8,9},{9,8},{10,11... | collective-permute-start | bytes 1179656 | tf_op jit(solution)/shard_map/ppermute | solution.py:20
  52.6 19.7 %collective-permute-start.14 = (bf16[192,512]{1,0:T(8,128)(2,1)S(1)}, bf16[192,512]{1,0:T(8,128)(2,1)S(1)}, u32[]{:S(2)}, u32[]{:S(2)}) collective-permute-start(bf16[192,512]{1,0:T(8,128)(2,1)S(1)} %get-tuple-element.15), channel_id=1, source_target_pairs={{32,0},{64,32},{96,64},{128,96},{160,128},{192,160},{224,192},{256... | collective-permute-start | bytes 589832 | tf_op jit(solution)/shard_map/ppermute | solution.py:16
  72.4 28.2 %collective-permute-start = (bf16[1,2,192,512]{3,2,1,0:T(8,128)(2,1)S(1)}, bf16[1,2,192,512]{3,2,1,0:T(8,128)(2,1)S(1)}, u32[]{:S(2)}, u32[]{:S(2)}) collective-permute-start(bf16[1,2,192,512]{3,2,1,0:T(8,128)(2,1)S(1)} %copy-done.3), channel_id=1, source_target_pairs={{480,0},{0,32},{32,64},{64,96},{96,128},{128,160},{160,192},{192,2... | collective-permute-start | bytes 1179656 | tf_op jit(solution)/shard_map/ppermute | solution.py:16
  76.9 36.6 %collective-permute-start.18 = (bf16[2,2,192,512]{3,2,1,0:T(8,128)(2,1)S(1)}, bf16[2,2,192,512]{3,2,1,0:T(8,128)(2,1)S(1)}, u32[]{:S(2)}, u32[]{:S(2)}) collective-permute-start(bf16[2,2,192,512]{3,2,1,0:T(8,128)(2,1)S(1)} %get-tuple-element.19), channel_id=1, source_target_pairs={{0,1},{1,0},{2,3},{3,2},{4,5},{5,4},{6,7},{7,6},{8,9},{9,8},{10,11... | collective-permute-start | bytes 2359304 | tf_op jit(solution)/shard_map/ppermute | solution.py:20
  78.8 36.7 %collective-permute-start.21 = (bf16[2,192,512]{2,1,0:T(8,128)(2,1)S(1)}, bf16[2,192,512]{2,1,0:T(8,128)(2,1)S(1)}, u32[]{:S(2)}, u32[]{:S(2)}) collective-permute-start(bf16[2,192,512]{2,1,0:T(8,128)(2,1)S(1)} %get-tuple-element.21), channel_id=1, source_target_pairs={{24,0},{0,8},{8,16},{16,24},{25,1},{1,9},{9,17},{17,25},{26,2},{2,... | collective-permute-start | bytes 1179656 | tf_op jit(solution)/shard_map/ppermute | solution.py:16
  100.6 11.5 %collective-permute-start.1 = (bf16[192,512]{1,0:T(8,128)(2,1)S(1)}, bf16[192,512]{1,0:T(8,128)(2,1)S(1)}, u32[]{:S(2)}, u32[]{:S(2)}) collective-permute-start(bf16[192,512]{1,0:T(8,128)(2,1)S(1)} %slice_bitcast_fusion.first), channel_id=1, source_target_pairs={{0,4},{1,5},{2,6},{3,7},{4,0},{5,1},{6,2},{7,3},{8,12},{9,13},{10,... | collective-permute-start | bytes 589832 | tf_op jit(solution)/shard_map/ppermute | solution.py:20
  102.5 16.9 %collective-permute-start.22 = (bf16[2,192,512]{2,1,0:T(8,128)(2,1)S(1)}, bf16[2,192,512]{2,1,0:T(8,128)(2,1)S(1)}, u32[]{:S(2)}, u32[]{:S(2)}) collective-permute-start(bf16[2,192,512]{2,1,0:T(8,128)(2,1)S(1)} %get-tuple-element.22), channel_id=1, source_target_pairs={{16,0},{24,8},{0,16},{8,24},{17,1},{25,9},{1,17},{9,25},{18,2},{26... | collective-permute-start | bytes 1179656 | tf_op jit(solution)/shard_map/ppermute | solution.py:16
  105.8 18.0 %collective-permute-start.23 = (bf16[2,192,512]{2,1,0:T(8,128)(2,1)S(1)}, bf16[2,192,512]{2,1,0:T(8,128)(2,1)S(1)}, u32[]{:S(2)}, u32[]{:S(2)}) collective-permute-start(bf16[2,192,512]{2,1,0:T(8,128)(2,1)S(1)} %get-tuple-element.23), channel_id=1, source_target_pairs={{8,0},{16,8},{24,16},{0,24},{9,1},{17,9},{25,17},{1,25},{10,2},{18... | collective-permute-start | bytes 1179656 | tf_op jit(solution)/shard_map/ppermute | solution.py:16
  112.1 15.4 %collective-permute-start.16 = (bf16[2,192,512]{2,1,0:T(8,128)(2,1)S(1)}, bf16[2,192,512]{2,1,0:T(8,128)(2,1)S(1)}, u32[]{:S(2)}, u32[]{:S(2)}) collective-permute-start(bf16[2,192,512]{2,1,0:T(8,128)(2,1)S(1)} %get-tuple-element.17), channel_id=1, source_target_pairs={{0,288},{256,32},{1,289},{257,33},{2,290},{258,34},{3,291},{259,35... | collective-permute-start | bytes 1179656 | tf_op jit(solution)/shard_map/ppermute | solution.py:202
  113.5 14.8 %collective-permute-start.2 = (bf16[2,192,512]{2,1,0:T(8,128)(2,1)S(1)}, bf16[2,192,512]{2,1,0:T(8,128)(2,1)S(1)}, u32[]{:S(2)}, u32[]{:S(2)}) collective-permute-start(bf16[2,192,512]{2,1,0:T(8,128)(2,1)S(1)} %shard_map.84.mine_a), channel_id=1, source_target_pairs={{0,2},{1,3},{2,0},{3,1},{4,6},{5,7},{6,4},{7,5},{8,10},{9,11},{10,... | collective-permute-start | bytes 1179656 | tf_op jit(solution)/shard_map/ppermute | solution.py:20
  115.5 19.2 %collective-permute-start.19 = (bf16[2,192,512]{2,1,0:T(8,128)(2,1)S(1)}, bf16[2,192,512]{2,1,0:T(8,128)(2,1)S(1)}, u32[]{:S(2)}, u32[]{:S(2)}) collective-permute-start(bf16[2,192,512]{2,1,0:T(8,128)(2,1)S(1)} %shard_map.90), channel_id=1, source_target_pairs={{0,2},{1,3},{2,0},{3,1},{4,6},{5,7},{6,4},{7,5},{8,10},{9,11},{10,... | collective-permute-start | bytes 1179656 | tf_op jit(solution)/shard_map/ppermute | solution.py:20
  123.9 23.0 %collective-permute-start.24 = (bf16[3,192,512]{2,1,0:T(8,128)(2,1)S(1)}, bf16[3,192,512]{2,1,0:T(8,128)(2,1)S(1)}, u32[]{:S(2)}, u32[]{:S(2)}) collective-permute-start(bf16[3,192,512]{2,1,0:T(8,128)(2,1)S(1)} %shard_map.93), channel_id=1, source_target_pairs={{0,1},{1,0},{2,3},{3,2},{4,5},{5,4},{6,7},{7,6},{8,9},{9,8},{10,11... | collective-permute-start | bytes 1769480 | tf_op jit(solution)/shard_map/ppermute | solution.py:20
  125.8 13.9 %collective-permute-start.15 = (bf16[2,192,512]{2,1,0:T(8,128)(2,1)S(1)}, bf16[2,192,512]{2,1,0:T(8,128)(2,1)S(1)}, u32[]{:S(2)}, u32[]{:S(2)}) collective-permute-start(bf16[2,192,512]{2,1,0:T(8,128)(2,1)S(1)} %get-tuple-element.17), channel_id=1, source_target_pairs={{32,0},{64,32},{96,64},{128,96},{160,128},{192,160},{224,192},{288... | collective-permute-start | bytes 1179656 | tf_op jit(solution)/shard_map/ppermute | solution.py:203
  127.5 16.7 %collective-permute-start.17 = (bf16[2,192,512]{2,1,0:T(8,128)(2,1)S(1)}, bf16[2,192,512]{2,1,0:T(8,128)(2,1)S(1)}, u32[]{:S(2)}, u32[]{:S(2)}) collective-permute-start(bf16[2,192,512]{2,1,0:T(8,128)(2,1)S(1)} %collective-permute-done.16), channel_id=1, source_target_pairs={{288,480},{32,224},{289,481},{33,225},{290,482},{34,226},{291,483}... | collective-permute-start | bytes 1179656 | tf_op jit(solution)/shard_map/ppermute | solution.py:204
  128.2 16.8 %collective-permute-start.3 = (bf16[2,192,512]{2,1,0:T(8,128)(2,1)S(1)}, bf16[2,192,512]{2,1,0:T(8,128)(2,1)S(1)}, u32[]{:S(2)}, u32[]{:S(2)}) collective-permute-start(bf16[2,192,512]{2,1,0:T(8,128)(2,1)S(1)} %shard_map.84.mine_a), channel_id=1, source_target_pairs={{0,1},{1,0},{2,3},{3,2},{4,5},{5,4},{6,7},{7,6},{8,9},{9,8},{10,11... | collective-permute-start | bytes 1179656 | tf_op jit(solution)/shard_map/ppermute | solution.py:20
  134.7 10.4 %collective-permute-start.4 = (bf16[2,192,512]{2,1,0:T(8,128)(2,1)S(1)}, bf16[2,192,512]{2,1,0:T(8,128)(2,1)S(1)}, u32[]{:S(2)}, u32[]{:S(2)}) collective-permute-start(bf16[2,192,512]{2,1,0:T(8,128)(2,1)S(1)} %collective-permute-done.2.mine_b), channel_id=1, source_target_pairs={{0,1},{1,0},{2,3},{3,2},{4,5},{5,4},{6,7},{7,6},{8,9},{9,8},{10,11... | collective-permute-start | bytes 1179656 | tf_op jit(solution)/shard_map/ppermute | solution.py:20
  139.7 13.0 %collective-permute-start.20 = (bf16[192,512]{1,0:T(8,128)(2,1)S(1)}, bf16[192,512]{1,0:T(8,128)(2,1)S(1)}, u32[]{:S(2)}, u32[]{:S(2)}) collective-permute-start(bf16[192,512]{1,0:T(8,128)(2,1)S(1)} %shard_map.91), channel_id=1, source_target_pairs={{0,4},{1,5},{2,6},{3,7},{4,0},{5,1},{6,2},{7,3},{8,12},{9,13},{10,... | collective-permute-start | bytes 589832 | tf_op jit(solution)/shard_map/ppermute | solution.py:20

commit v3 on v2

--- a/solution.py
+++ b/solution.py
@@ -100,10 +100,10 @@
         send_out[which, at] = send
 
 
-def new_kernel(mine_a, mine_b, other_a, other_b, own, prev, nxt, far_lo, far_hi, inbound, out):
+def new_kernel(mine_a, mine_b, other_a, other_b, own, prev, nxt, far_lo, far_hi, upper, lower, out):
     pre = project((mine_a, mine_b), (other_a, other_b), shards(own, prev, nxt, far_lo, far_hi))
-    out[0, 0] = (inbound[0, 1].astype(F32) + pre * jax.nn.sigmoid(pre)).astype(BF16)
-    out[0, 1] = inbound[0, 0]
+    out[0, 0] = (lower[...].astype(F32) + pre * jax.nn.sigmoid(pre)).astype(BF16)
+    out[0, 1] = upper[...]
 
 
 def split_kernel(back, grad, held_out, grad_out, late_out):
@@ -195,7 +195,8 @@
     nxt = shifted(own, "dp", -1)
     held_out, grad_out, late_out = run(split_kernel, (block, block, two), (sent_back, sent_grad))
     back_lower = shifted(held_out, "section", -1)
-    inbound = shifted(sent_out, "section", 1)
+    upper_in = shifted(sent_out[0, 0], "section", 1)
+    lower_in = shifted(sent_out[0, 1], "section", 1)
     grad_upper = shifted(grad_out, "section", -1)
     count = lax.axis_size("section")
     rank = count // 2
@@ -205,7 +206,6 @@
     far_lo = shifted(prev[:half], "dp", 1)
     far_hi = shifted(nxt[half:], "dp", -1)
     weights = (own, prev, nxt, far_lo, far_hi)
-    upper_in = inbound[0, 0]
     held = gathered(back_lower)
     new = gathered(upper_in)
 
@@ -224,7 +224,7 @@
         from_dp.append(shifted(to_dp[distance - 1], "dp", distance))
     near_sum = run(near_kernel, shape((2, tokens, width), BF16), (keep, received))
     near = exchanged(near_sum, 2)
-    emitted = run(new_kernel, pair, (*new, *weights, inbound), flops=product, mib=16)
+    emitted = run(new_kernel, pair, (*new, *weights, upper_in, lower_in), flops=product, mib=16)
     far_sum = run(far_kernel, shape((tokens, width), BF16), (keep, received, near))
     far = exchanged(far_sum, 4)
     rebuilt = run(rebuilt_kernel, pair, (pre_held, back_lower, late, late_wrap), flops=tokens * width)

time: 154 us -> 168 us (1.091)
  the two profiles are of different devices: /device:TPU:6 before, /device:TPU:1 now
where the time goes in v3:
time: 168 us; the launch traced here: 167 us
  starting transfers between devices  103 us (61%)
  waiting for transfers between devices  52 us (31%)
  Pallas kernels  8.37 us (5%)
  local copies, waits for them, and re-layouts  2.1 us (1%)
  between operations  1.68 us (1%)
    ppermute x11, starting transfers between devices, shifted(): return lax.ppermute(block, axis, route)  66.2 us
    ppermute x12, starting transfers between devices, exchanged(): lax.ppermute(block, 'tensor', [(i, i ^ flip) for i in range(lax.axis_size...  33.3 us
    ppermute x11, waiting for transfers between devices, shifted(): return lax.ppermute(block, axis, route)  27.8 us
    ppermute x12, waiting for transfers between devices, exchanged(): lax.ppermute(block, 'tensor', [(i, i ^ flip) for i in range(lax.axis_size...  22 us
    pallas_call x11, Pallas kernels, run(): pl.pallas_call(kernel, out_shape=outs, in_specs=[smem if n < scalars else...  8.37 us
  transfers between devices with their start and end apart: 26, of which 10 were waited for; matrix products, arithmetic and copies ran while one was open for 0% of the time, Pallas kernels for 3%

profile of v3, /device:TPU:1, one launch (start us, length us, event | category | flops | bytes accessed | tf_op | source)
XLA Modules:
  0.0 166.9 jit_solution(5675065876177610295)
XLA Ops:
  0.6 3.9 %collective-permute-start.5 = (bf16[1024,512]{1,0:T(8,128)(2,1)}, bf16[1024,512]{1,0:T(8,128)(2,1)S(1)}, u32[]{:S(2)}, u32[]{:S(2)}) collective-permute-start(bf16[1024,512]{1,0:T(8,128)(2,1)} %bitcast.5), channel_id=1, source_target_pairs={{24,0},{0,8},{8,16},{16,24},{25,1},{1,9},{9,17},{17,25},{26,2},{2,... | collective-permute-start | bytes 3145736 | tf_op jit(solution)/shard_map/ppermute | solution.py:16
  4.6 3.2 %collective-permute-start.6 = (bf16[1024,512]{1,0:T(8,128)(2,1)}, bf16[1024,512]{1,0:T(8,128)(2,1)S(1)}, u32[]{:S(2)}, u32[]{:S(2)}) collective-permute-start(bf16[1024,512]{1,0:T(8,128)(2,1)} %bitcast.6), channel_id=1, source_target_pairs={{8,0},{16,8},{24,16},{0,24},{9,1},{17,9},{25,17},{1,25},{10,2},{18... | collective-permute-start | bytes 3145736 | tf_op jit(solution)/shard_map/ppermute | solution.py:16
  7.8 1.0 copy-done.1
  8.8 1.0 copy-done.2
  9.8 0.1 shard_map.86
  9.8 13.7 %collective-permute-start.10 = (bf16[192,512]{1,0:T(8,128)(2,1)S(1)}, bf16[192,512]{1,0:T(8,128)(2,1)S(1)}, u32[]{:S(2)}, u32[]{:S(2)}) collective-permute-start(bf16[192,512]{1,0:T(8,128)(2,1)S(1)} %get-tuple-element.14), channel_id=1, source_target_pairs={{32,0},{64,32},{96,64},{128,96},{160,128},{192,160},{224,192},{256... | collective-permute-start | bytes 589832 | tf_op jit(solution)/shard_map/ppermute | solution.py:16
  23.6 3.4 %collective-permute-done.10.first.lower = bf16[192,512]{1,0:T(8,128)(2,1)S(1)} collective-permute-done((bf16[192,512]{1,0:T(8,128)(2,1)S(1)}, bf16[192,512]{1,0:T(8,128)(2,1)S(1)}, u32[]{:S(2)}, u32[]{:S(2)}) %collective-permute-start.10) | collective-permute-done | bytes 196640 | tf_op jit(solution)/shard_map/ppermute | solution.py:16
  27.0 3.8 %collective-permute-start.11 = (bf16[192,512]{1,0:T(8,128)(2,1)S(1)}, bf16[192,512]{1,0:T(8,128)(2,1)S(1)}, u32[]{:S(2)}, u32[]{:S(2)}) collective-permute-start(bf16[192,512]{1,0:T(8,128)(2,1)S(1)} %collective-permute-done.10.first.lower), channel_id=1, source_target_pairs={{0,4},{1,5},{2,6},{3,7},{4,0},{5,1},{6,2},{7,3},{8,12},{9,13},{10,... | collective-permute-start | bytes 589832 | tf_op jit(solution)/shard_map/ppermute | solution.py:20
  30.7 9.1 %collective-permute-done.11.second = bf16[192,512]{1,0:T(8,128)(2,1)S(1)} collective-permute-done((bf16[192,512]{1,0:T(8,128)(2,1)S(1)}, bf16[192,512]{1,0:T(8,128)(2,1)S(1)}, u32[]{:S(2)}, u32[]{:S(2)}) %collective-permute-start.11) | collective-permute-done | bytes 196640 | tf_op jit(solution)/shard_map/ppermute | solution.py:20
  39.9 0.0 copy-start
  39.9 2.5 %collective-permute-start.12 = (bf16[2,192,512]{2,1,0:T(8,128)(2,1)S(1)}, bf16[2,192,512]{2,1,0:T(8,128)(2,1)S(1)}, u32[]{:S(2)}, u32[]{:S(2)}) collective-permute-start(bf16[2,192,512]{2,1,0:T(8,128)(2,1)S(1)} %shard_map.87.mine_a), channel_id=1, source_target_pairs={{0,2},{1,3},{2,0},{3,1},{4,6},{5,7},{6,4},{7,5},{8,10},{9,11},{10,... | collective-permute-start | bytes 1179656 | tf_op jit(solution)/shard_map/ppermute | solution.py:20
  42.5 1.9 %collective-permute-start.7 = (bf16[512,512]{1,0:T(8,128)(2,1)S(1)}, bf16[512,512]{1,0:T(8,128)(2,1)S(1)}, u32[]{:S(2)}, u32[]{:S(2)}) collective-permute-start(bf16[512,512]{1,0:T(8,128)(2,1)S(1)} %slice.16), channel_id=1, source_target_pairs={{24,0},{0,8},{8,16},{16,24},{25,1},{1,9},{9,17},{17,25},{26,2},{2,... | collective-permute-start | bytes 1572872 | tf_op jit(solution)/shard_map/ppermute | solution.py:16
  44.5 4.6 %collective-permute-start.8 = (bf16[512,512]{1,0:T(8,128)(2,1)S(1)}, bf16[512,512]{1,0:T(8,128)(2,1)S(1)}, u32[]{:S(2)}, u32[]{:S(2)}) collective-permute-start(bf16[512,512]{1,0:T(8,128)(2,1)S(1)} %slice.17), channel_id=1, source_target_pairs={{8,0},{16,8},{24,16},{0,24},{9,1},{17,9},{25,17},{1,25},{10,2},{18... | collective-permute-start | bytes 1572872 | tf_op jit(solution)/shard_map/ppermute | solution.py:16
  49.0 3.6 %collective-permute-start.13 = (bf16[2,192,512]{2,1,0:T(8,128)(2,1)S(1)}, bf16[2,192,512]{2,1,0:T(8,128)(2,1)S(1)}, u32[]{:S(2)}, u32[]{:S(2)}) collective-permute-start(bf16[2,192,512]{2,1,0:T(8,128)(2,1)S(1)} %shard_map.87.mine_a), channel_id=1, source_target_pairs={{0,1},{1,0},{2,3},{3,2},{4,5},{5,4},{6,7},{7,6},{8,9},{9,8},{10,11... | collective-permute-start | bytes 1179656 | tf_op jit(solution)/shard_map/ppermute | solution.py:20
  52.6 2.7 %collective-permute-start.14 = (bf16[2,192,512]{2,1,0:T(8,128)(2,1)S(1)}, bf16[2,192,512]{2,1,0:T(8,128)(2,1)S(1)}, u32[]{:S(2)}, u32[]{:S(2)}) collective-permute-start(bf16[2,192,512]{2,1,0:T(8,128)(2,1)S(1)} %collective-permute-done.12.mine_b), channel_id=1, source_target_pairs={{0,1},{1,0},{2,3},{3,2},{4,5},{5,4},{6,7},{7,6},{8,9},{9,8},{10,11... | collective-permute-start | bytes 1179656 | tf_op jit(solution)/shard_map/ppermute | solution.py:20
  55.3 13.0 %collective-permute-start.15 = (bf16[192,512]{1,0:T(8,128)(2,1)S(1)}, bf16[192,512]{1,0:T(8,128)(2,1)S(1)}, u32[]{:S(2)}, u32[]{:S(2)}) collective-permute-start(bf16[192,512]{1,0:T(8,128)(2,1)S(1)} %get-tuple-element.15), channel_id=1, source_target_pairs={{32,0},{64,32},{96,64},{128,96},{160,128},{192,160},{224,192},{256... | collective-permute-start | bytes 589832 | tf_op jit(solution)/shard_map/ppermute | solution.py:16
  69.0 0.0 copy-start.3
  69.0 4.8 %collective-permute-done.15.grad.upper = bf16[192,512]{1,0:T(8,128)(2,1)S(1)} collective-permute-done((bf16[192,512]{1,0:T(8,128)(2,1)S(1)}, bf16[192,512]{1,0:T(8,128)(2,1)S(1)}, u32[]{:S(2)}, u32[]{:S(2)}) %collective-permute-start.15) | collective-permute-done | bytes 196640 | tf_op jit(solution)/shard_map/ppermute | solution.py:16
  73.9 2.5 %shard_map.88 = (bf16[2,2,192,512]{3,2,1,0:T(8,128)(2,1)S(1)}, bf16[2,2,192,512]{3,2,1,0:T(8,128)(2,1)S(1)}, bf16[3,192,512]{2,1,0:T(8,128)(2,1)S(1)}, bf16[2,19...) custom-call(s32[1,1]{1,0:T(1,128)S(6)} %copy.9.length, ...), custom_call_target="tpu_custom_call" | custom-call | flops 1610612736 | bytes 5963780 | tf_op jit(solution)/shard_map/pallas_call | solution.py:163
  76.4 3.1 %collective-permute-start.19 = (bf16[2,2,192,512]{3,2,1,0:T(8,128)(2,1)S(1)}, bf16[2,2,192,512]{3,2,1,0:T(8,128)(2,1)S(1)}, u32[]{:S(2)}, u32[]{:S(2)}) collective-permute-start(bf16[2,2,192,512]{3,2,1,0:T(8,128)(2,1)S(1)} %get-tuple-element.19), channel_id=1, source_target_pairs={{0,1},{1,0},{2,3},{3,2},{4,5},{5,4},{6,7},{7,6},{8,9},{9,8},{10,11... | collective-permute-start | bytes 2359304 | tf_op jit(solution)/shard_map/ppermute | solution.py:20
  79.6 1.9 %collective-permute-start = (bf16[192,512]{1,0:T(8,128)(2,1)S(1)}, bf16[192,512]{1,0:T(8,128)(2,1)S(1)}, u32[]{:S(2)}, u32[]{:S(2)}) collective-permute-start(bf16[192,512]{1,0:T(8,128)(2,1)S(1)} %get-tuple-element.25), channel_id=1, source_target_pairs={{480,0},{0,32},{32,64},{64,96},{96,128},{128,160},{160,192},{192,2... | collective-permute-start | bytes 589832 | tf_op jit(solution)/shard_map/ppermute | solution.py:16
  81.5 1.9 %collective-permute-start.22 = (bf16[2,192,512]{2,1,0:T(8,128)(2,1)S(1)}, bf16[2,192,512]{2,1,0:T(8,128)(2,1)S(1)}, u32[]{:S(2)}, u32[]{:S(2)}) collective-permute-start(bf16[2,192,512]{2,1,0:T(8,128)(2,1)S(1)} %get-tuple-element.21), channel_id=1, source_target_pairs={{24,0},{0,8},{8,16},{16,24},{25,1},{1,9},{9,17},{17,25},{26,2},{2,... | collective-permute-start | bytes 1179656 | tf_op jit(solution)/shard_map/ppermute | solution.py:16
  83.4 17.4 %collective-permute-done.first.upper = bf16[192,512]{1,0:T(8,128)(2,1)S(1)} collective-permute-done((bf16[192,512]{1,0:T(8,128)(2,1)S(1)}, bf16[192,512]{1,0:T(8,128)(2,1)S(1)}, u32[]{:S(2)}, u32[]{:S(2)}) %collective-permute-start) | collective-permute-done | bytes 196640 | tf_op jit(solution)/shard_map/ppermute | solution.py:16
  100.9 1.9 %collective-permute-start.1 = (bf16[192,512]{1,0:T(8,128)(2,1)S(1)}, bf16[192,512]{1,0:T(8,128)(2,1)S(1)}, u32[]{:S(2)}, u32[]{:S(2)}) collective-permute-start(bf16[192,512]{1,0:T(8,128)(2,1)S(1)} %collective-permute-done.first.upper), channel_id=1, source_target_pairs={{0,4},{1,5},{2,6},{3,7},{4,0},{5,1},{6,2},{7,3},{8,12},{9,13},{10,... | collective-permute-start | bytes 589832 | tf_op jit(solution)/shard_map/ppermute | solution.py:20
  102.8 2.3 %collective-permute-start.23 = (bf16[2,192,512]{2,1,0:T(8,128)(2,1)S(1)}, bf16[2,192,512]{2,1,0:T(8,128)(2,1)S(1)}, u32[]{:S(2)}, u32[]{:S(2)}) collective-permute-start(bf16[2,192,512]{2,1,0:T(8,128)(2,1)S(1)} %get-tuple-element.22), channel_id=1, source_target_pairs={{16,0},{24,8},{0,16},{8,24},{17,1},{25,9},{1,17},{9,25},{18,2},{26... | collective-permute-start | bytes 1179656 | tf_op jit(solution)/shard_map/ppermute | solution.py:16
  105.1 2.8 %collective-permute-start.24 = (bf16[2,192,512]{2,1,0:T(8,128)(2,1)S(1)}, bf16[2,192,512]{2,1,0:T(8,128)(2,1)S(1)}, u32[]{:S(2)}, u32[]{:S(2)}) collective-permute-start(bf16[2,192,512]{2,1,0:T(8,128)(2,1)S(1)} %get-tuple-element.23), channel_id=1, source_target_pairs={{8,0},{16,8},{24,16},{0,24},{9,1},{17,9},{25,17},{1,25},{10,2},{18... | collective-permute-start | bytes 1179656 | tf_op jit(solution)/shard_map/ppermute | solution.py:16
  107.9 5.2 %collective-permute-done.1.second = bf16[192,512]{1,0:T(8,128)(2,1)S(1)} collective-permute-done((bf16[192,512]{1,0:T(8,128)(2,1)S(1)}, bf16[192,512]{1,0:T(8,128)(2,1)S(1)}, u32[]{:S(2)}, u32[]{:S(2)}) %collective-permute-start.1) | collective-permute-done | bytes 196640 | tf_op jit(solution)/shard_map/ppermute | solution.py:20
  113.1 1.3 collective-permute-start.17
  114.4 1.3 collective-permute-start.16
  115.7 1.9 %collective-permute-start.2 = (bf16[2,192,512]{2,1,0:T(8,128)(2,1)S(1)}, bf16[2,192,512]{2,1,0:T(8,128)(2,1)S(1)}, u32[]{:S(2)}, u32[]{:S(2)}) collective-permute-start(bf16[2,192,512]{2,1,0:T(8,128)(2,1)S(1)} %shard_map.84.mine_a), channel_id=1, source_target_pairs={{0,2},{1,3},{2,0},{3,1},{4,6},{5,7},{6,4},{7,5},{8,10},{9,11},{10,... | collective-permute-start | bytes 1179656 | tf_op jit(solution)/shard_map/ppermute | solution.py:20
  117.7 0.1 shard_map.90
  117.8 3.4 %collective-permute-start.20 = (bf16[2,192,512]{2,1,0:T(8,128)(2,1)S(1)}, bf16[2,192,512]{2,1,0:T(8,128)(2,1)S(1)}, u32[]{:S(2)}, u32[]{:S(2)}) collective-permute-start(bf16[2,192,512]{2,1,0:T(8,128)(2,1)S(1)} %shard_map.90), channel_id=1, source_target_pairs={{0,2},{1,3},{2,0},{3,1},{4,6},{5,7},{6,4},{7,5},{8,10},{9,11},{10,... | collective-permute-start | bytes 1179656 | tf_op jit(solution)/shard_map/ppermute | solution.py:20
  121.1 1.3 collective-permute-done.24.dp_3
  122.4 3.5 %collective-permute-start.25 = (bf16[3,192,512]{2,1,0:T(8,128)(2,1)S(1)}, bf16[3,192,512]{2,1,0:T(8,128)(2,1)S(1)}, u32[]{:S(2)}, u32[]{:S(2)}) collective-permute-start(bf16[3,192,512]{2,1,0:T(8,128)(2,1)S(1)} %shard_map.93), channel_id=1, source_target_pairs={{0,1},{1,0},{2,3},{3,2},{4,5},{5,4},{6,7},{7,6},{8,9},{9,8},{10,11... | collective-permute-start | bytes 1769480 | tf_op jit(solution)/shard_map/ppermute | solution.py:20
  125.9 2.2 %collective-permute-done.17 = bf16[2,192,512]{2,1,0:T(8,128)(2,1)S(1)} collective-permute-done((bf16[2,192,512]{2,1,0:T(8,128)(2,1)S(1)}, bf16[2,192,512]{2,1,0:T(8,128)(2,1)S(1)}, u32[]{:S(2)}, u32[]{:S(2)}) %collective-permute-start.17) | collective-permute-done | bytes 393248 | tf_op jit(solution)/shard_map/ppermute | solution.py:203
  128.1 0.7 collective-permute-start.18
  128.8 3.1 %collective-permute-start.3 = (bf16[2,192,512]{2,1,0:T(8,128)(2,1)S(1)}, bf16[2,192,512]{2,1,0:T(8,128)(2,1)S(1)}, u32[]{:S(2)}, u32[]{:S(2)}) collective-permute-start(bf16[2,192,512]{2,1,0:T(8,128)(2,1)S(1)} %shard_map.84.mine_a), channel_id=1, source_target_pairs={{0,1},{1,0},{2,3},{3,2},{4,5},{5,4},{6,7},{7,6},{8,9},{9,8},{10,11... | collective-permute-start | bytes 1179656 | tf_op jit(solution)/shard_map/ppermute | solution.py:20
  132.0 1.9 %collective-permute-start.4 = (bf16[2,192,512]{2,1,0:T(8,128)(2,1)S(1)}, bf16[2,192,512]{2,1,0:T(8,128)(2,1)S(1)}, u32[]{:S(2)}, u32[]{:S(2)}) collective-permute-start(bf16[2,192,512]{2,1,0:T(8,128)(2,1)S(1)} %collective-permute-done.2.mine_b), channel_id=1, source_target_pairs={{0,1},{1,0},{2,3},{3,2},{4,5},{5,4},{6,7},{7,6},{8,9},{9,8},{10,11... | collective-permute-start | bytes 1179656 | tf_op jit(solution)/shard_map/ppermute | solution.py:20
  133.9 2.3 %collective-permute-done.20.near = bf16[2,192,512]{2,1,0:T(8,128)(2,1)S(1)} collective-permute-done((bf16[2,192,512]{2,1,0:T(8,128)(2,1)S(1)}, bf16[2,192,512]{2,1,0:T(8,128)(2,1)S(1)}, u32[]{:S(2)}, u32[]{:S(2)}) %collective-permute-start.20) | collective-permute-done | bytes 393248 | tf_op jit(solution)/shard_map/ppermute | solution.py:20
  136.2 16.8 %collective-permute-start.9 = (bf16[192,512]{1,0:T(8,128)(2,1)S(1)}, bf16[192,512]{1,0:T(8,128)(2,1)S(1)}, u32[]{:S(2)}, u32[]{:S(2)}) collective-permute-start(bf16[192,512]{1,0:T(8,128)(2,1)S(1)} %get-tuple-element.24), channel_id=1, source_target_pairs={{480,0},{0,32},{32,64},{64,96},{96,128},{128,160},{160,192},{192,2... | collective-permute-start | bytes 589832 | tf_op jit(solution)/shard_map/ppermute | solution.py:16
  153.1 0.1 shard_map.91
  153.2 1.9 %collective-permute-start.21 = (bf16[192,512]{1,0:T(8,128)(2,1)S(1)}, bf16[192,512]{1,0:T(8,128)(2,1)S(1)}, u32[]{:S(2)}, u32[]{:S(2)}) collective-permute-start(bf16[192,512]{1,0:T(8,128)(2,1)S(1)} %shard_map.91), channel_id=1, source_target_pairs={{0,4},{1,5},{2,6},{3,7},{4,0},{5,1},{6,2},{7,3},{8,12},{9,13},{10,... | collective-permute-start | bytes 589832 | tf_op jit(solution)/shard_map/ppermute | solution.py:20
  155.1 0.8 shard_map.89
  155.9 0.9 collective-permute-done.9.lower
  156.8 1.8 %shard_map.85 = bf16[1,2,192,512]{3,2,1,0:T(8,128)(2,1)} custom-call(bf16[2,192,512]{2,1,0:T(8,128)(2,1)S(1)} %shard_map.84.mine_a, bf16[2,192,512]{2,1,0:T(8,128)(2,1)S(1)} %collective-permute-done.2.mine_b, bf16[2,192,512]{2,1,0:T(8,128)(2,1)S(1)} %collective-permute-done.3.other_a, bf16[2,192,512]{2,1,0:T(8,128)(2,1)S(1)} %collective-permute-done.4.other_b, ...), custom_call_target="tpu_custom_call" | custom-call | flops 805306368 | bytes 6160384 | tf_op jit(solution)/shard_map/pallas_call | solution.py:163
  158.6 2.0 %shard_map.94 = bf16[1,1024,512]{2,1,0:T(8,128)(2,1)} custom-call(bf16[3,192,512]{2,1,0:T(8,128)(2,1)S(1)} %get-tuple-element.20.own, bf16[2,192,512]{2,1,0:T(8,128)(2,1)S(1)} %collective-permute-done.22.dp_1, bf16[2,192,512]{2,1,0:T(8,128)(2,1)S(1)} %collective-permute-done.23.dp_2, bf16[2,192,512]{2,1,0:T(8,128)(2,1)S(1)} %collective-permute-done.24.dp_3, ...), custom_call_target="tpu_custom_call" | custom-call | flops 805306368 | bytes 2359296 | tf_op jit(solution)/shard_map/pallas_call | solution.py:163
  160.6 5.4 %collective-permute-done.21.far = bf16[192,512]{1,0:T(8,128)(2,1)S(1)} collective-permute-done((bf16[192,512]{1,0:T(8,128)(2,1)S(1)}, bf16[192,512]{1,0:T(8,128)(2,1)S(1)}, u32[]{:S(2)}, u32[]{:S(2)}) %collective-permute-start.21) | collective-permute-done | bytes 196640 | tf_op jit(solution)/shard_map/ppermute | solution.py:20
  166.0 0.9 shard_map.92
  (26 shorter events, 0.2 us)
Async XLA Ops:
  0.6 41.8 %collective-permute-start.5 = (bf16[1024,512]{1,0:T(8,128)(2,1)}, bf16[1024,512]{1,0:T(8,128)(2,1)S(1)}, u32[]{:S(2)}, u32[]{:S(2)}) collective-permute-start(bf16[1024,512]{1,0:T(8,128)(2,1)} %bitcast.5), channel_id=1, source_target_pairs={{24,0},{0,8},{8,16},{16,24},{25,1},{1,9},{9,17},{17,25},{26,2},{2,... | collective-permute-start | bytes 3145736 | tf_op jit(solution)/shard_map/ppermute | solution.py:16
  4.6 39.8 %collective-permute-start.6 = (bf16[1024,512]{1,0:T(8,128)(2,1)}, bf16[1024,512]{1,0:T(8,128)(2,1)S(1)}, u32[]{:S(2)}, u32[]{:S(2)}) collective-permute-start(bf16[1024,512]{1,0:T(8,128)(2,1)} %bitcast.6), channel_id=1, source_target_pairs={{8,0},{16,8},{24,16},{0,24},{9,1},{17,9},{25,17},{1,25},{10,2},{18... | collective-permute-start | bytes 3145736 | tf_op jit(solution)/shard_map/ppermute | solution.py:16
  7.8 1.0 copy-start.1
  8.8 1.0 copy-start.2
  9.8 17.1 %collective-permute-start.10 = (bf16[192,512]{1,0:T(8,128)(2,1)S(1)}, bf16[192,512]{1,0:T(8,128)(2,1)S(1)}, u32[]{:S(2)}, u32[]{:S(2)}) collective-permute-start(bf16[192,512]{1,0:T(8,128)(2,1)S(1)} %get-tuple-element.14), channel_id=1, source_target_pairs={{32,0},{64,32},{96,64},{128,96},{160,128},{192,160},{224,192},{256... | collective-permute-start | bytes 589832 | tf_op jit(solution)/shard_map/ppermute | solution.py:16
  27.0 12.9 %collective-permute-start.11 = (bf16[192,512]{1,0:T(8,128)(2,1)S(1)}, bf16[192,512]{1,0:T(8,128)(2,1)S(1)}, u32[]{:S(2)}, u32[]{:S(2)}) collective-permute-start(bf16[192,512]{1,0:T(8,128)(2,1)S(1)} %collective-permute-done.10.first.lower), channel_id=1, source_target_pairs={{0,4},{1,5},{2,6},{3,7},{4,0},{5,1},{6,2},{7,3},{8,12},{9,13},{10,... | collective-permute-start | bytes 589832 | tf_op jit(solution)/shard_map/ppermute | solution.py:20
  39.9 34.0 %copy-start = (bf16[1,1024,512]{2,1,0:T(8,128)(2,1)S(1)}, bf16[1,1024,512]{2,1,0:T(8,128)(2,1)}, u32[]{:S(2)}) copy-start(bf16[1,1024,512]{2,1,0:T(8,128)(2,1)} %param.9) | copy-start | bytes 3145732
  39.9 12.8 %collective-permute-start.12 = (bf16[2,192,512]{2,1,0:T(8,128)(2,1)S(1)}, bf16[2,192,512]{2,1,0:T(8,128)(2,1)S(1)}, u32[]{:S(2)}, u32[]{:S(2)}) collective-permute-start(bf16[2,192,512]{2,1,0:T(8,128)(2,1)S(1)} %shard_map.87.mine_a), channel_id=1, source_target_pairs={{0,2},{1,3},{2,0},{3,1},{4,6},{5,7},{6,4},{7,5},{8,10},{9,11},{10,... | collective-permute-start | bytes 1179656 | tf_op jit(solution)/shard_map/ppermute | solution.py:20
  42.5 31.4 %collective-permute-start.7 = (bf16[512,512]{1,0:T(8,128)(2,1)S(1)}, bf16[512,512]{1,0:T(8,128)(2,1)S(1)}, u32[]{:S(2)}, u32[]{:S(2)}) collective-permute-start(bf16[512,512]{1,0:T(8,128)(2,1)S(1)} %slice.16), channel_id=1, source_target_pairs={{24,0},{0,8},{8,16},{16,24},{25,1},{1,9},{9,17},{17,25},{26,2},{2,... | collective-permute-start | bytes 1572872 | tf_op jit(solution)/shard_map/ppermute | solution.py:16
  44.5 29.4 %collective-permute-start.8 = (bf16[512,512]{1,0:T(8,128)(2,1)S(1)}, bf16[512,512]{1,0:T(8,128)(2,1)S(1)}, u32[]{:S(2)}, u32[]{:S(2)}) collective-permute-start(bf16[512,512]{1,0:T(8,128)(2,1)S(1)} %slice.17), channel_id=1, source_target_pairs={{8,0},{16,8},{24,16},{0,24},{9,1},{17,9},{25,17},{1,25},{10,2},{18... | collective-permute-start | bytes 1572872 | tf_op jit(solution)/shard_map/ppermute | solution.py:16
  49.0 24.8 %collective-permute-start.13 = (bf16[2,192,512]{2,1,0:T(8,128)(2,1)S(1)}, bf16[2,192,512]{2,1,0:T(8,128)(2,1)S(1)}, u32[]{:S(2)}, u32[]{:S(2)}) collective-permute-start(bf16[2,192,512]{2,1,0:T(8,128)(2,1)S(1)} %shard_map.87.mine_a), channel_id=1, source_target_pairs={{0,1},{1,0},{2,3},{3,2},{4,5},{5,4},{6,7},{7,6},{8,9},{9,8},{10,11... | collective-permute-start | bytes 1179656 | tf_op jit(solution)/shard_map/ppermute | solution.py:20
  52.6 21.2 %collective-permute-start.14 = (bf16[2,192,512]{2,1,0:T(8,128)(2,1)S(1)}, bf16[2,192,512]{2,1,0:T(8,128)(2,1)S(1)}, u32[]{:S(2)}, u32[]{:S(2)}) collective-permute-start(bf16[2,192,512]{2,1,0:T(8,128)(2,1)S(1)} %collective-permute-done.12.mine_b), channel_id=1, source_target_pairs={{0,1},{1,0},{2,3},{3,2},{4,5},{5,4},{6,7},{7,6},{8,9},{9,8},{10,11... | collective-permute-start | bytes 1179656 | tf_op jit(solution)/shard_map/ppermute | solution.py:20
  55.3 18.5 %collective-permute-start.15 = (bf16[192,512]{1,0:T(8,128)(2,1)S(1)}, bf16[192,512]{1,0:T(8,128)(2,1)S(1)}, u32[]{:S(2)}, u32[]{:S(2)}) collective-permute-start(bf16[192,512]{1,0:T(8,128)(2,1)S(1)} %get-tuple-element.15), channel_id=1, source_target_pairs={{32,0},{64,32},{96,64},{128,96},{160,128},{192,160},{224,192},{256... | collective-permute-start | bytes 589832 | tf_op jit(solution)/shard_map/ppermute | solution.py:16
  69.0 10.5 %copy-start.3 = (bf16[1,2,192,512]{3,2,1,0:T(8,128)(2,1)S(1)}, bf16[1,2,192,512]{3,2,1,0:T(8,128)(2,1)}, u32[]{:S(2)}) copy-start(bf16[1,2,192,512]{3,2,1,0:T(8,128)(2,1)} %param.5) | copy-start | bytes 1179652
  76.4 39.3 %collective-permute-start.19 = (bf16[2,2,192,512]{3,2,1,0:T(8,128)(2,1)S(1)}, bf16[2,2,192,512]{3,2,1,0:T(8,128)(2,1)S(1)}, u32[]{:S(2)}, u32[]{:S(2)}) collective-permute-start(bf16[2,2,192,512]{3,2,1,0:T(8,128)(2,1)S(1)} %get-tuple-element.19), channel_id=1, source_target_pairs={{0,1},{1,0},{2,3},{3,2},{4,5},{5,4},{6,7},{7,6},{8,9},{9,8},{10,11... | collective-permute-start | bytes 2359304 | tf_op jit(solution)/shard_map/ppermute | solution.py:20
  79.6 21.3 %collective-permute-start = (bf16[192,512]{1,0:T(8,128)(2,1)S(1)}, bf16[192,512]{1,0:T(8,128)(2,1)S(1)}, u32[]{:S(2)}, u32[]{:S(2)}) collective-permute-start(bf16[192,512]{1,0:T(8,128)(2,1)S(1)} %get-tuple-element.25), channel_id=1, source_target_pairs={{480,0},{0,32},{32,64},{64,96},{96,128},{128,160},{160,192},{192,2... | collective-permute-start | bytes 589832 | tf_op jit(solution)/shard_map/ppermute | solution.py:16
  81.5 32.9 %collective-permute-start.22 = (bf16[2,192,512]{2,1,0:T(8,128)(2,1)S(1)}, bf16[2,192,512]{2,1,0:T(8,128)(2,1)S(1)}, u32[]{:S(2)}, u32[]{:S(2)}) collective-permute-start(bf16[2,192,512]{2,1,0:T(8,128)(2,1)S(1)} %get-tuple-element.21), channel_id=1, source_target_pairs={{24,0},{0,8},{8,16},{16,24},{25,1},{1,9},{9,17},{17,25},{26,2},{2,... | collective-permute-start | bytes 1179656 | tf_op jit(solution)/shard_map/ppermute | solution.py:16
  100.9 12.2 %collective-permute-start.1 = (bf16[192,512]{1,0:T(8,128)(2,1)S(1)}, bf16[192,512]{1,0:T(8,128)(2,1)S(1)}, u32[]{:S(2)}, u32[]{:S(2)}) collective-permute-start(bf16[192,512]{1,0:T(8,128)(2,1)S(1)} %collective-permute-done.first.upper), channel_id=1, source_target_pairs={{0,4},{1,5},{2,6},{3,7},{4,0},{5,1},{6,2},{7,3},{8,12},{9,13},{10,... | collective-permute-start | bytes 589832 | tf_op jit(solution)/shard_map/ppermute | solution.py:20
  102.8 15.0 %collective-permute-start.23 = (bf16[2,192,512]{2,1,0:T(8,128)(2,1)S(1)}, bf16[2,192,512]{2,1,0:T(8,128)(2,1)S(1)}, u32[]{:S(2)}, u32[]{:S(2)}) collective-permute-start(bf16[2,192,512]{2,1,0:T(8,128)(2,1)S(1)} %get-tuple-element.22), channel_id=1, source_target_pairs={{16,0},{24,8},{0,16},{8,24},{17,1},{25,9},{1,17},{9,25},{18,2},{26... | collective-permute-start | bytes 1179656 | tf_op jit(solution)/shard_map/ppermute | solution.py:16
  105.1 17.3 %collective-permute-start.24 = (bf16[2,192,512]{2,1,0:T(8,128)(2,1)S(1)}, bf16[2,192,512]{2,1,0:T(8,128)(2,1)S(1)}, u32[]{:S(2)}, u32[]{:S(2)}) collective-permute-start(bf16[2,192,512]{2,1,0:T(8,128)(2,1)S(1)} %get-tuple-element.23), channel_id=1, source_target_pairs={{8,0},{16,8},{24,16},{0,24},{9,1},{17,9},{25,17},{1,25},{10,2},{18... | collective-permute-start | bytes 1179656 | tf_op jit(solution)/shard_map/ppermute | solution.py:16
  113.1 15.1 %collective-permute-start.17 = (bf16[2,192,512]{2,1,0:T(8,128)(2,1)S(1)}, bf16[2,192,512]{2,1,0:T(8,128)(2,1)S(1)}, u32[]{:S(2)}, u32[]{:S(2)}) collective-permute-start(bf16[2,192,512]{2,1,0:T(8,128)(2,1)S(1)} %get-tuple-element.17), channel_id=1, source_target_pairs={{0,288},{256,32},{1,289},{257,33},{2,290},{258,34},{3,291},{259,35... | collective-permute-start | bytes 1179656 | tf_op jit(solution)/shard_map/ppermute | solution.py:203
  114.4 14.4 %collective-permute-start.16 = (bf16[2,192,512]{2,1,0:T(8,128)(2,1)S(1)}, bf16[2,192,512]{2,1,0:T(8,128)(2,1)S(1)}, u32[]{:S(2)}, u32[]{:S(2)}) collective-permute-start(bf16[2,192,512]{2,1,0:T(8,128)(2,1)S(1)} %get-tuple-element.17), channel_id=1, source_target_pairs={{32,0},{64,32},{96,64},{128,96},{160,128},{192,160},{224,192},{288... | collective-permute-start | bytes 1179656 | tf_op jit(solution)/shard_map/ppermute | solution.py:204
  115.7 16.2 %collective-permute-start.2 = (bf16[2,192,512]{2,1,0:T(8,128)(2,1)S(1)}, bf16[2,192,512]{2,1,0:T(8,128)(2,1)S(1)}, u32[]{:S(2)}, u32[]{:S(2)}) collective-permute-start(bf16[2,192,512]{2,1,0:T(8,128)(2,1)S(1)} %shard_map.84.mine_a), channel_id=1, source_target_pairs={{0,2},{1,3},{2,0},{3,1},{4,6},{5,7},{6,4},{7,5},{8,10},{9,11},{10,... | collective-permute-start | bytes 1179656 | tf_op jit(solution)/shard_map/ppermute | solution.py:20
  117.8 18.5 %collective-permute-start.20 = (bf16[2,192,512]{2,1,0:T(8,128)(2,1)S(1)}, bf16[2,192,512]{2,1,0:T(8,128)(2,1)S(1)}, u32[]{:S(2)}, u32[]{:S(2)}) collective-permute-start(bf16[2,192,512]{2,1,0:T(8,128)(2,1)S(1)} %shard_map.90), channel_id=1, source_target_pairs={{0,2},{1,3},{2,0},{3,1},{4,6},{5,7},{6,4},{7,5},{8,10},{9,11},{10,... | collective-permute-start | bytes 1179656 | tf_op jit(solution)/shard_map/ppermute | solution.py:20
  122.4 36.1 %collective-permute-start.25 = (bf16[3,192,512]{2,1,0:T(8,128)(2,1)S(1)}, bf16[3,192,512]{2,1,0:T(8,128)(2,1)S(1)}, u32[]{:S(2)}, u32[]{:S(2)}) collective-permute-start(bf16[3,192,512]{2,1,0:T(8,128)(2,1)S(1)} %shard_map.93), channel_id=1, source_target_pairs={{0,1},{1,0},{2,3},{3,2},{4,5},{5,4},{6,7},{7,6},{8,9},{9,8},{10,11... | collective-permute-start | bytes 1769480 | tf_op jit(solution)/shard_map/ppermute | solution.py:20
  128.1 25.0 %collective-permute-start.18 = (bf16[2,192,512]{2,1,0:T(8,128)(2,1)S(1)}, bf16[2,192,512]{2,1,0:T(8,128)(2,1)S(1)}, u32[]{:S(2)}, u32[]{:S(2)}) collective-permute-start(bf16[2,192,512]{2,1,0:T(8,128)(2,1)S(1)} %collective-permute-done.17), channel_id=1, source_target_pairs={{288,480},{32,224},{289,481},{33,225},{290,482},{34,226},{291,483}... | collective-permute-start | bytes 1179656 | tf_op jit(solution)/shard_map/ppermute | solution.py:205
  128.8 28.0 %collective-permute-start.3 = (bf16[2,192,512]{2,1,0:T(8,128)(2,1)S(1)}, bf16[2,192,512]{2,1,0:T(8,128)(2,1)S(1)}, u32[]{:S(2)}, u32[]{:S(2)}) collective-permute-start(bf16[2,192,512]{2,1,0:T(8,128)(2,1)S(1)} %shard_map.84.mine_a), channel_id=1, source_target_pairs={{0,1},{1,0},{2,3},{3,2},{4,5},{5,4},{6,7},{7,6},{8,9},{9,8},{10,11... | collective-permute-start | bytes 1179656 | tf_op jit(solution)/shard_map/ppermute | solution.py:20
  132.0 24.8 %collective-permute-start.4 = (bf16[2,192,512]{2,1,0:T(8,128)(2,1)S(1)}, bf16[2,192,512]{2,1,0:T(8,128)(2,1)S(1)}, u32[]{:S(2)}, u32[]{:S(2)}) collective-permute-start(bf16[2,192,512]{2,1,0:T(8,128)(2,1)S(1)} %collective-permute-done.2.mine_b), channel_id=1, source_target_pairs={{0,1},{1,0},{2,3},{3,2},{4,5},{5,4},{6,7},{7,6},{8,9},{9,8},{10,11... | collective-permute-start | bytes 1179656 | tf_op jit(solution)/shard_map/ppermute | solution.py:20
  136.2 20.6 %collective-permute-start.9 = (bf16[192,512]{1,0:T(8,128)(2,1)S(1)}, bf16[192,512]{1,0:T(8,128)(2,1)S(1)}, u32[]{:S(2)}, u32[]{:S(2)}) collective-permute-start(bf16[192,512]{1,0:T(8,128)(2,1)S(1)} %get-tuple-element.24), channel_id=1, source_target_pairs={{480,0},{0,32},{32,64},{64,96},{96,128},{128,160},{160,192},{192,2... | collective-permute-start | bytes 589832 | tf_op jit(solution)/shard_map/ppermute | solution.py:16
  153.2 12.8 %collective-permute-start.21 = (bf16[192,512]{1,0:T(8,128)(2,1)S(1)}, bf16[192,512]{1,0:T(8,128)(2,1)S(1)}, u32[]{:S(2)}, u32[]{:S(2)}) collective-permute-start(bf16[192,512]{1,0:T(8,128)(2,1)S(1)} %shard_map.91), channel_id=1, source_target_pairs={{0,4},{1,5},{2,6},{3,7},{4,0},{5,1},{6,2},{7,3},{8,12},{9,13},{10,... | collective-permute-start | bytes 589832 | tf_op jit(solution)/shard_map/ppermute | solution.py:20
